TPU v7x, 256 devices: a whole 4x4x8 slice. The times are simulated.
256 devices in a mesh: dp: 4 (over x_hi, core), mp: 64 (over x_lo, y, z).
Axes of the slice: x: 4 (x_hi: 2, x_lo: 2; x = x_hi * 2 + x_lo), y: 4, z: 8, core: 2. Of those that a mesh axis runs over, the one named last changes fastest.
Arguments:
- source_prompts: bfloat16 [128, 64, 4096], P(None, None, 'mp'), may hold values from -6 to 6
- task_logits: float32 [8, 128], replicated, may hold values from -8 to 260
- task_ids: int32 [256], P('dp'), may hold values from 0 to 7
- key_weight: bfloat16 [4096, 4096], P(None, 'mp'), may hold values from -0.09375 to 0.09375
- value_weight: bfloat16 [4096, 4096], P(None, 'mp'), may hold values from -0.09375 to 0.09375
- queries: bfloat16 [256, 128, 4096], P(('dp', 'mp')), may hold values from -32 to 32
- keys: bfloat16 [256, 128, 4096], P(('dp', 'mp')), may hold values from -16 to 16
- values: bfloat16 [256, 128, 4096], P(('dp', 'mp')), may hold values from -6 to 6
- cotangent: bfloat16 [256, 128, 4096], P(('dp', 'mp')), may hold values from -6 to 6
Outputs:
- attended: bfloat16 [256, 128, 4096], P(('dp', 'mp'))
- source_grad: float32 [128, 64, 4096], P(None, 'dp', 'mp')
- logits_grad: float32 [8, 128], replicated
All inputs are finite; a program needn't handle non-finite values.
Results may differ from a plain program's by a relative error of at most 0.011.
Values may be sent and summed in bfloat16 or wider, within the bound.
A program may use at most 128 MiB of HBM per device.

v0:
```python
import jax
import jax.numpy as jnp
from jax import lax
from jax.sharding import Mesh
from jax.sharding import PartitionSpec as P

D = 4096
HEADS = 32
DH = 128
NSRC = 128
NTASK = 8
PTOK = 64
SEQ = 128
DP = ("dp_0", "dp_1")
MP = ("mp_0", "mp_1", "mp_2")
DP_MP = ("dp_0", "dp_1", "mp_0", "mp_1", "mp_2")


mask_fill = -1e30


def in_order(blocks, dim):
    blocks = jnp.moveaxis(blocks, 0, dim)
    lengths = blocks.shape
    return blocks.reshape(*lengths[:dim], lengths[dim] * lengths[dim + 1], *lengths[dim + 2 :])


def all_blocks(array, axes, turns):
    blocks = array[None]
    for k in turns:
        blocks = lax.all_gather(blocks, axes[k], axis=0, tiled=True)
    held = [lax.axis_size(axes[k]) for k in reversed(turns)]
    blocks = blocks.reshape(*held, *array.shape)
    turned = sorted(range(len(turns)), key=lambda place: turns[len(turns) - 1 - place])
    return blocks.transpose(*turned, *range(len(turns), blocks.ndim)).reshape(-1, *array.shape)


def whole_of(array, axes, turns, dim):
    return in_order(all_blocks(array, axes, turns), dim)


def cut_along(array, dim, peers):
    before, after = (array.shape[:dim], array.shape[dim + 1 :])
    return jnp.moveaxis(array.reshape(*before, peers, -1, *after), dim, 0)


def sum_at_owner(array, axis, dim):
    blocks = cut_along(array, dim, lax.axis_size(axis))
    arrived = lax.all_to_all(blocks, axis, split_axis=0, concat_axis=0, tiled=True)
    return arrived.astype(jnp.float32).sum(axis=0)


def one_axis_at_a_time(array, axes):
    for axis in axes:
        array = lax.psum(array, axis)
    return array


def example_block(prompt_pair, queries, keys, values, cotangent):
    examples = queries.shape[0]
    score_scale = DH ** (-0.5)
    key_all = jnp.concatenate([prompt_pair[:, :, 0, :], keys], axis=1)
    value_all = jnp.concatenate([prompt_pair[:, :, 1, :], values], axis=1)
    query_heads = queries.reshape(examples, SEQ, HEADS, DH)
    key_heads = key_all.reshape(examples, PTOK + SEQ, HEADS, DH)
    value_heads = value_all.reshape(examples, PTOK + SEQ, HEADS, DH)
    cot_heads = cotangent.reshape(examples, SEQ, HEADS, DH)
    scores = (
        jnp.einsum("eihd,ejhd->ehij", query_heads, key_heads, preferred_element_type=jnp.float32)
        * score_scale
    )
    column = jnp.arange(PTOK + SEQ)[None, :]
    position = jnp.arange(SEQ)[:, None]
    visible = (column < PTOK) | (column - PTOK <= position)
    scores = jnp.where(visible[None, None], scores, mask_fill)
    top_score = jnp.max(scores, axis=3, keepdims=True)
    exponent = jnp.exp(scores - top_score)
    attention = exponent / jnp.sum(exponent, axis=3, keepdims=True)
    attention_rounded = attention.astype(jnp.bfloat16)
    attended = jnp.einsum(
        "ehij,ejhd->eihd", attention_rounded, value_heads, preferred_element_type=jnp.float32
    )
    attended = attended.astype(jnp.bfloat16).reshape(examples, SEQ, D)
    grad_attention = jnp.einsum(
        "eihd,ejhd->ehij", cot_heads, value_heads, preferred_element_type=jnp.float32
    )
    inner_sum = jnp.sum(attention * grad_attention, axis=3, keepdims=True)
    grad_scores = (attention * (grad_attention - inner_sum)).astype(jnp.bfloat16)
    key_grads = jnp.einsum(
        "ehij,eihd->ejhd",
        grad_scores[:, :, :, :PTOK],
        query_heads,
        preferred_element_type=jnp.float32,
    )
    key_grads = (key_grads * score_scale).astype(jnp.bfloat16).reshape(examples, PTOK, D)
    value_grads = jnp.einsum(
        "ehij,eihd->ejhd",
        attention_rounded[:, :, :, :PTOK],
        cot_heads,
        preferred_element_type=jnp.float32,
    )
    value_grads = value_grads.astype(jnp.bfloat16).reshape(examples, PTOK, D)
    return (attended, jnp.stack([key_grads, value_grads], axis=2))


def tile_products(tile_grad, source_prompts, mix_weights, col_width):
    rows_here = tile_grad.shape[1]
    own_prompts = lax.dynamic_slice_in_dim(
        source_prompts, lax.axis_index(DP) * rows_here, rows_here, 1
    )
    tile_flat = tile_grad.reshape(NTASK, rows_here * col_width)
    source_grad = jnp.dot(mix_weights.T, tile_flat, precision=lax.Precision.HIGHEST)
    source_grad = source_grad.reshape(NSRC, rows_here, col_width)
    weight_part = jnp.dot(
        tile_flat,
        own_prompts.reshape(NSRC, rows_here * col_width).astype(jnp.float32).T,
        precision=lax.Precision.HIGHEST,
    )
    return (source_grad, weight_part)


def on_device(
    source_prompts,
    task_logits,
    task_ids,
    key_weight,
    value_weight,
    queries,
    keys,
    values,
    cotangent,
):
    col_width = key_weight.shape[1]
    group_examples = task_ids.shape[0]
    mix_weights = jax.nn.softmax(task_logits, axis=1)
    mix_rounded = mix_weights.astype(jnp.bfloat16)
    mixture = jnp.dot(
        mix_rounded,
        source_prompts.reshape(NSRC, PTOK * col_width),
        preferred_element_type=jnp.float32,
    )
    mixture = mixture.astype(jnp.bfloat16).reshape(NTASK, PTOK, col_width)
    pair_weight = jnp.concatenate([key_weight, value_weight], axis=1)
    portion = whole_of(mixture, MP, (0, 1, 2), 2)
    portion_rows = portion.reshape(NTASK * PTOK, portion.shape[2])
    projected = jnp.dot(portion_rows, pair_weight, preferred_element_type=jnp.float32)
    projected = projected.astype(jnp.bfloat16).reshape(NTASK, PTOK, 2, col_width)
    task_range = jnp.arange(NTASK, dtype=jnp.int32)
    selector_all = (task_ids[:, None] == task_range[None, :]).astype(jnp.bfloat16)
    outgoing = jnp.dot(
        selector_all,
        projected.reshape(NTASK, PTOK * 2 * col_width),
        preferred_element_type=jnp.float32,
    )
    outgoing = outgoing.astype(jnp.bfloat16).reshape(group_examples, PTOK, 2, col_width)
    prompt_pair = lax.all_to_all(outgoing, MP, split_axis=0, concat_axis=3, tiled=True)
    attended, outgoing_grads = example_block(prompt_pair, queries, keys, values, cotangent)
    incoming = lax.all_to_all(outgoing_grads, MP, split_axis=3, concat_axis=0, tiled=True)
    group_grads = jnp.dot(
        selector_all.T,
        incoming.reshape(group_examples, PTOK * 2 * col_width),
        preferred_element_type=jnp.float32,
    )
    pair_weight_t = pair_weight.astype(jnp.float32).T
    task_rows = sum_at_owner(
        group_grads.reshape(NTASK, PTOK, 2 * col_width).astype(jnp.bfloat16), DP, 1
    )
    rows_here = task_rows.shape[1]
    row_terms = jnp.dot(
        task_rows.reshape(NTASK * rows_here, 2 * col_width),
        pair_weight_t,
        precision=lax.Precision.HIGHEST,
    ).reshape(NTASK, rows_here, D)
    tile_grad = sum_at_owner(row_terms.astype(jnp.bfloat16), MP, 2)
    source_grad, weight_part = tile_products(tile_grad, source_prompts, mix_weights, col_width)
    weight_grad = one_axis_at_a_time(weight_part, DP_MP)
    logits_grad = mix_weights * (
        weight_grad - jnp.sum(mix_weights * weight_grad, axis=1, keepdims=True)
    )
    return (attended, source_grad, logits_grad)


def solution(mesh):
    torus = Mesh(mesh.devices.reshape(2, 2, 2, 4, 8), ("dp_0", "dp_1", "mp_0", "mp_1", "mp_2"))
    return jax.shard_map(
        on_device,
        mesh=torus,
        in_specs=(
            P(None, None, MP),
            P(),
            P(DP),
            P(None, MP),
            P(None, MP),
            P(DP_MP, None, None),
            P(DP_MP, None, None),
            P(DP_MP, None, None),
            P(DP_MP, None, None),
        ),
        out_specs=(P(DP_MP, None, None), P(None, DP, MP), P()),
        check_vma=False,
    )
```

profile of v0, /device:TPU:8, one launch (start us, length us, event | category | flops | bytes accessed | tf_op | source)
XLA Modules:
  0.0 423.8 jit_solution(2100457335903616325)
XLA Ops:
  10.3 5.9 %all_gather.9 = bf16[2,8,64,64]{3,2,1,0:T(8,128)(2,1)S(1)} all-gather(bf16[1,8,64,64]{3,2,1,0:T(8,128)(2,1)S(1)} %broadcast_in_dim_reshape.3), channel_id=1, replica_groups=mesh['dp_0'=2,'dp_1'=2,'mp_0'=2,'mp_1'=4,'mp_2'=8] {'mp_0'}, dimensions={0}, use_global_device_ids=true | all-gather | bytes 196608 | tf_op jit(solution)/shard_map/all_gather | solution.py:31
  16.2 16.1 %all_gather.10 = bf16[8,8,64,64]{3,2,1,0:T(8,128)(2,1)} all-gather(bf16[2,8,64,64]{3,2,1,0:T(8,128)(2,1)S(1)} %all_gather.9), channel_id=1, replica_groups=mesh['dp_0'=2,'dp_1'=2,'mp_0'=2,'mp_1'=4,'mp_2'=8] {'mp_1'}, dimensions={0}, use_global_device_ids=true | all-gather | bytes 655360 | tf_op jit(solution)/shard_map/all_gather | solution.py:31
  34.8 94.3 %all-gather.2.cloned.1.call-done = bf16[64,8,64,64]{3,2,1,0:T(8,128)(2,1)} async-done(((bf16[8,8,64,64]{3,2,1,0:T(8,128)(2,1)}), bf16[64,8,64,64]{3,2,1,0:T(8,128)(2,1)}) %all-gather.2.cloned.1.call-update) | async-done | bytes 4194320 | tf_op jit(solution)/shard_map/all_gather | solution.py:31
  129.1 10.3 %copy.68 = bf16[2,4,8,8,64,64]{5,4,3,2,1,0:T(8,128)(2,1)} copy(bf16[2,4,8,8,64,64]{5,4,3,0,1,2:T(8,128)(2,1)} %bitcast.156) | data formatting | bytes 8388608 | tf_op jit(solution)/shard_map/transpose | solution.py:35
  139.4 12.0 %copy.69 = bf16[8,64,64,64]{3,2,1,0:T(8,128)(2,1)} copy(bf16[8,64,64,64]{3,1,0,2:T(8,128)(2,1)} %bitcast.150) | data formatting | bytes 8388608 | tf_op jit(solution)/shard_map/transpose | solution.py:23
  151.4 12.3 %reshape_reshape.6 = bf16[512,4096]{1,0:T(8,128)(2,1)} reshape(bf16[8,64,64,64]{3,2,1,0:T(8,128)(2,1)} %copy.69) | data formatting | bytes 8388608 | tf_op jit(solution)/shard_map/reshape;reshape | solution.py:145
  168.7 4.4 %reshape.173 = bf16[64,64,2,64]{3,2,1,0:T(2,128)(2,1)S(1)} reshape(bf16[64,8192]{1,0:T(8,128)(2,1)} %convolution_convert_fusion) | data formatting | bytes 2097152 | tf_op jit(solution)/shard_map/reshape | solution.py:155
  175.1 4.8 %reshape.189 = bf16[64,2,4096]{2,1,0:T(2,128)(2,1)} reshape(bf16[64,2,64,64]{3,2,1,0:T(8,128)(2,1)} %bitcast.157) | data formatting | bytes 2097152
  179.9 9.6 %all-to-all-start = ((bf16[64,2,4096]{2,1,0:T(2,128)(2,1)}), bf16[64,2,4096]{2,1,0:T(2,128)(2,1)}, u32[]{:S(2)}, u32[]{:S(2)}) async-start(bf16[64,2,4096]{2,1,0:T(2,128)(2,1)} %reshape.189), calls=%async_computation | async-start | bytes 2097152 | tf_op jit(solution)/shard_map/all_to_all | solution.py:156
  197.2 20.5 %all-to-all-done = bf16[64,2,4096]{2,1,0:T(2,128)(2,1)} async-done(((bf16[64,2,4096]{2,1,0:T(2,128)(2,1)}), bf16[64,2,4096]{2,1,0:T(2,128)(2,1)}, u32[]{:S(2)}, u32[]{:S(2)}) %all-to-all-start) | async-done | bytes 1048608 | tf_op jit(solution)/shard_map/all_to_all | solution.py:156
  217.7 4.8 %reshape.190 = bf16[64,2,64,64]{3,2,1,0:T(8,128)(2,1)} reshape(bf16[64,2,4096]{2,1,0:T(2,128)(2,1)} %all-to-all-done) | data formatting | bytes 2097152
  251.4 5.3 %reshape.191 = bf16[64,2,4096]{2,1,0:T(2,128)(2,1)S(1)} reshape(bf16[4096,1,2,64]{3,2,1,0:T(2,128)(2,1)} %bitcast.155) | data formatting | bytes 2097152
  256.7 33.9 %all_to_all.43 = bf16[64,2,4096]{2,1,0:T(2,128)(2,1)} all-to-all(bf16[64,2,4096]{2,1,0:T(2,128)(2,1)S(1)} %reshape.191), channel_id=1, replica_groups=mesh['dp_0'=2,'dp_1'=2,'mp_0'=2,'mp_1'=4,'mp_2'=8] {'mp_0','mp_1','mp_2'}, dimensions={0} | all-to-all | bytes 2097152 | tf_op jit(solution)/shard_map/all_to_all | solution.py:158
  290.6 5.8 %reshape.192 = bf16[4096,1,2,64]{3,2,1,0:T(2,128)(2,1)} reshape(bf16[64,2,4096]{2,1,0:T(2,128)(2,1)} %all_to_all.43) | data formatting | bytes 2097152
  296.4 8.0 %copy.90 = bf16[1,64,2,64,64]{4,2,1,3,0:T(2,128)(2,1)} copy(bf16[1,64,2,64,64]{1,2,4,3,0:T(2,128)(2,1)} %bitcast.158) | data formatting | bytes 2097152 | tf_op jit(solution)/shard_map/all_to_all | solution.py:158
  304.4 5.3 %reshape.181 = bf16[64,8192]{1,0:T(8,128)(2,1)S(1)} reshape(bf16[64,1,64,2,64]{4,3,2,0,1:T(2,128)(2,1)} %bitcast.159) | data formatting | bytes 2097152 | tf_op jit(solution)/shard_map/reshape | solution.py:161
  309.9 9.9 %all_to_all.44 = bf16[4,8,16,128]{3,1,2,0:T(8,128)(2,1)S(1)} all-to-all(bf16[4,8,16,128]{3,1,2,0:T(8,128)(2,1)S(1)} %bitcast.170), channel_id=1, replica_groups=mesh['dp_0'=2,'dp_1'=2,'mp_0'=2,'mp_1'=4,'mp_2'=8] {'dp_0','dp_1'}, dimensions={0} | all-to-all | bytes 262144 | tf_op jit(solution)/shard_map/all_to_all | solution.py:49
  330.3 4.7 %reshape.193 = bf16[64,2,4096]{2,1,0:T(2,128)(2,1)} reshape(bf16[64,8,16,64]{3,2,1,0:T(8,128)(2,1)} %bitcast.160) | data formatting | bytes 2097152
  335.0 6.5 %all-to-all-start.3 = ((bf16[64,2,4096]{2,1,0:T(2,128)(2,1)}), bf16[64,2,4096]{2,1,0:T(2,128)(2,1)}, u32[]{:S(2)}, u32[]{:S(2)}) async-start(bf16[64,2,4096]{2,1,0:T(2,128)(2,1)} %reshape.193), calls=%async_computation.3 | async-start | bytes 2097152 | tf_op jit(solution)/shard_map/all_to_all | solution.py:49
  347.4 22.6 %all-to-all-done.3 = bf16[64,2,4096]{2,1,0:T(2,128)(2,1)} async-done(((bf16[64,2,4096]{2,1,0:T(2,128)(2,1)}), bf16[64,2,4096]{2,1,0:T(2,128)(2,1)}, u32[]{:S(2)}, u32[]{:S(2)}) %all-to-all-start.3) | async-done | bytes 1048608 | tf_op jit(solution)/shard_map/all_to_all | solution.py:49
  374.6 6.4 %psum.35 = f32[8,128]{1,0:T(8,128)S(1)} all-reduce(f32[8,128]{1,0:T(8,128)S(1)} %convolution_bitcast_fusion), channel_id=1, replica_groups=mesh['dp_0'=2,'dp_1'=2,'mp_0'=2,'mp_1'=4,'mp_2'=8] {'dp_0'}, use_global_device_ids=true, to_apply=%region_7.8 | all-reduce | flops 1024 | bytes 8192 | tf_op jit(solution)/shard_map/psum | solution.py:55
  383.5 4.9 %psum.37 = f32[8,128]{1,0:T(8,128)S(1)} all-reduce(f32[8,128]{1,0:T(8,128)S(1)} %psum.36), channel_id=1, replica_groups=mesh['dp_0'=2,'dp_1'=2,'mp_0'=2,'mp_1'=4,'mp_2'=8] {'mp_0'}, use_global_device_ids=true, to_apply=%region_9.10 | all-reduce | flops 1024 | bytes 8192 | tf_op jit(solution)/shard_map/psum | solution.py:55
  388.4 9.1 %psum.38 = f32[8,128]{1,0:T(8,128)S(1)} all-reduce(f32[8,128]{1,0:T(8,128)S(1)} %psum.37), channel_id=1, replica_groups=mesh['dp_0'=2,'dp_1'=2,'mp_0'=2,'mp_1'=4,'mp_2'=8] {'mp_1'}, use_global_device_ids=true, to_apply=%region_10.11 | all-reduce | flops 1024 | bytes 8192 | tf_op jit(solution)/shard_map/psum | solution.py:55
  397.5 16.4 %psum.39 = f32[8,128]{1,0:T(8,128)S(1)} all-reduce(f32[8,128]{1,0:T(8,128)S(1)} %psum.38), channel_id=1, replica_groups=mesh['dp_0'=2,'dp_1'=2,'mp_0'=2,'mp_1'=4,'mp_2'=8] {'mp_2'}, use_global_device_ids=true, to_apply=%region_11.12 | all-reduce | flops 1024 | bytes 8192 | tf_op jit(solution)/shard_map/psum | solution.py:55
  (88 shorter events, 75.3 us)
Async XLA Ops:
  7.2 1.9 copy-start
  7.2 25.2 %copy-start.11 = (bf16[4096,64]{0,1:T(8,128)(2,1)S(1)}, bf16[4096,64]{0,1:T(8,128)(2,1)}, u32[]{:S(2)}) copy-start(bf16[4096,64]{0,1:T(8,128)(2,1)} %param.12) | copy-start | bytes 1572868
  7.2 121.9 %all-gather.2.cloned.1.call-start = ((), (), s32[]{:S(2)}) async-start(), calls=%async_computation.4 | async-start | bytes 9437184 | tf_op jit(solution)/shard_map/all_gather | solution.py:31
  32.8 130.8 %copy-start.3 = (bf16[4096,64]{1,0:T(8,128)(2,1)}, bf16[4096,64]{1,0:T(8,128)(2,1)S(1)}, u32[]{:S(2)}) copy-start(bf16[4096,64]{1,0:T(8,128)(2,1)S(1)} %copy.70) | copy-start | bytes 1572868
  34.8 128.9 %copy-start.4 = (bf16[4096,64]{1,0:T(8,128)(2,1)}, bf16[4096,64]{1,0:T(8,128)(2,1)S(1)}, u32[]{:S(2)}) copy-start(bf16[4096,64]{1,0:T(8,128)(2,1)S(1)} %copy.71) | copy-start | bytes 1572868
  163.7 3.6 copy-start.13
  175.1 14.4 %copy-start.9 = (bf16[1,128,4096]{2,1,0:T(8,128)(2,1)S(1)}, bf16[1,128,4096]{2,1,0:T(8,128)(2,1)}, u32[]{:S(2)}) copy-start(bf16[1,128,4096]{2,1,0:T(8,128)(2,1)} %param.14) | copy-start | bytes 3145732
  175.1 15.6 %copy-start.10 = (bf16[1,128,4096]{2,1,0:T(8,128)(2,1)S(1)}, bf16[1,128,4096]{2,1,0:T(8,128)(2,1)}, u32[]{:S(2)}) copy-start(bf16[1,128,4096]{2,1,0:T(8,128)(2,1)} %param.15) | copy-start | bytes 3145732
  179.9 37.8 %all-to-all-start = ((bf16[64,2,4096]{2,1,0:T(2,128)(2,1)}), bf16[64,2,4096]{2,1,0:T(2,128)(2,1)}, u32[]{:S(2)}, u32[]{:S(2)}) async-start(bf16[64,2,4096]{2,1,0:T(2,128)(2,1)} %reshape.189), calls=%async_computation | async-start | bytes 2097152 | tf_op jit(solution)/shard_map/all_to_all | solution.py:156
  231.2 2.8 copy-start.5
  231.2 2.9 copy-start.7
  233.0 0.8 copy-start.1
  235.7 2.9 copy-start.8
  235.7 2.0 copy-start.6
  330.3 12.6 %copy-start.2 = (bf16[8,8,32,128]{3,2,1,0:T(8,128)(2,1)S(1)}, bf16[8,8,32,128]{3,2,1,0:T(8,128)(2,1)}, u32[]{:S(2)}) copy-start(bf16[8,8,32,128]{3,2,1,0:T(8,128)(2,1)} %copy-done.1) | copy-start | bytes 1572868
  335.0 35.1 %all-to-all-start.3 = ((bf16[64,2,4096]{2,1,0:T(2,128)(2,1)}), bf16[64,2,4096]{2,1,0:T(2,128)(2,1)}, u32[]{:S(2)}, u32[]{:S(2)}) async-start(bf16[64,2,4096]{2,1,0:T(2,128)(2,1)} %reshape.193), calls=%async_computation.3 | async-start | bytes 2097152 | tf_op jit(solution)/shard_map/all_to_all | solution.py:49
  347.4 66.5 %copy-start.12 = (f32[8,128]{1,0:T(8,128)S(1)}, f32[8,128]{1,0:T(8,128)}, u32[]{:S(2)}) copy-start(f32[8,128]{1,0:T(8,128)} %param.10) | copy-start | bytes 12292
Sparse Core Ops, SparseCore 0:
  32.5 96.5 all-gather.1
where the time goes:
time: 432 us; the launch traced here: 424 us
  waiting for transfers between devices  137 us (32%)
  local copies, waits for them, and re-layouts  125 us (29%)
  blocking collectives  105 us (24%)
  matrix products  18.2 us (4%)
  starting transfers between devices  16.1 us (4%)
  between operations  14.6 us (3%)
  other arithmetic  7.71 us (2%)
    all_gather x1, waiting for transfers between devices, all_blocks(): blocks = lax.all_gather(blocks, axes[k], axis=0, tiled=True)  94.3 us
    unnamed x44, local copies, waits for them, and re-layouts  40.8 us
    psum x5, blocking collectives, one_axis_at_a_time(): array = lax.psum(array, axis)  39.3 us
    all_to_all x1, blocking collectives, on_device(): lax.all_to_all(outgoing_grads, MP, split_axis=3, concat_axis=0, tiled=True)  33.9 us
    all_to_all x1, waiting for transfers between devices, sum_at_owner(): lax.all_to_all(blocks, axis, split_axis=0, concat_axis=0, tiled=True)  22.6 us
    all_gather x2, blocking collectives, all_blocks(): blocks = lax.all_gather(blocks, axes[k], axis=0, tiled=True)  22 us
    all_to_all x1, waiting for transfers between devices, on_device(): lax.all_to_all(outgoing, MP, split_axis=0, concat_axis=3, tiled=True)  20.5 us
    another operation x1, local copies, waits for them, and re-layouts, on_device(): portion_rows = portion.reshape(NTASK * PTOK, portion.shape[2])  12.3 us
  transfers between devices with their start and end apart: 3, of which 3 were waited for; matrix products, arithmetic and copies ran while one was open for 4% of the time, Pallas kernels for 0%

commit v1 on v0

v1 whole, which is shorter than its diff:
```python
import functools

import jax
import jax.numpy as jnp
from jax import lax
from jax.experimental import pallas as pl
from jax.experimental.pallas import tpu as pltpu
from jax.sharding import Mesh
from jax.sharding import PartitionSpec as P

D = 4096
HEADS = 32
DH = 128
NSRC = 128
NTASK = 8
PTOK = 64
SEQ = 128
AXES = ("dp_0", "dp_1", "mp_0", "mp_1", "mp_2")
MP = ("mp_0", "mp_1", "mp_2")
DP = ("dp_0", "dp_1")
MESH = pl.DeviceIdType.MESH
ROWS = 16
COLS = 64
PLANE = 32
F32 = jnp.float32
BF16 = jnp.bfloat16
HIGH = lax.Precision.HIGHEST


def here():
    return tuple(lax.axis_index(name) for name in AXES)


def plane_index(a, c, x, y):
    return ((a * 2 + c) * 2 + x) * 4 + y


def plane_device(p):
    return {
        "dp_0": lax.div(p, 16),
        "dp_1": lax.rem(lax.div(p, 8), 2),
        "mp_0": lax.rem(lax.div(p, 4), 2),
        "mp_1": lax.rem(p, 4),
    }


def push(src, dst, sent, landed, device):
    return pltpu.make_async_remote_copy(
        src_ref=src, dst_ref=dst, send_sem=sent, recv_sem=landed, device_id=device, device_id_type=MESH
    )


def greet(me, z):
    barrier = pltpu.get_barrier_semaphore()

    def plane(o, carry):
        pl.semaphore_signal(barrier, inc=1, device_id=plane_device(lax.rem(me + o, PLANE)), device_id_type=MESH)
        return carry

    lax.fori_loop(1, PLANE, plane, 0)
    for o in range(1, 8):
        pl.semaphore_signal(barrier, inc=1, device_id={"mp_2": lax.rem(z + o, 8)}, device_id_type=MESH)
    pl.semaphore_wait(barrier, PLANE - 1 + 7)


def soft(logits):
    exponent = jnp.exp(logits - jnp.max(logits, axis=1, keepdims=True))
    return exponent / jnp.sum(exponent, axis=1, keepdims=True)


def block_of(p):
    return pl.ds(lax.rem(p, 8) * 4, 4), pl.ds(pl.multiple_of(lax.div(p, 8) * ROWS, ROWS), ROWS)


def forward_kernel(
    tids, logits, sp, kw, vw, pp, sel,
    mix_t, spv, w, tb, tt, out,
    load_sem, own_sem, xs, xr, zs, zr, ys, yr, us, ur, ts, tr, ps, pr,
):
    a, c, x, y, z = here()
    d = a * 2 + c
    me = plane_index(a, c, x, y)
    loads = (
        pltpu.make_async_copy(sp.at[pl.ds(d * ROWS, ROWS)], spv, load_sem.at[0]),
        pltpu.make_async_copy(kw, w.at[pl.ds(0, COLS)], load_sem.at[1]),
        pltpu.make_async_copy(vw, w.at[pl.ds(COLS, COLS)], load_sem.at[2]),
    )
    for load in loads:
        load.start()
    tt[me] = jnp.full((8, 128), tids[x * 32 + y * 8 + z], jnp.int32).astype(F32)
    tile = jnp.concatenate([soft(logits[...]).astype(BF16).astype(F32)] * ROWS, axis=0)
    row = lax.broadcasted_iota(jnp.int32, (128, 128), 0)
    loads[0].wait()
    total = jnp.zeros((COLS, 128), F32)
    for r in range(ROWS):
        weights = jnp.where(row // NTASK == r, tile, 0.0).astype(BF16)
        total += lax.dot_general(spv[r], weights, (((1,), (1,)), ((), ())), preferred_element_type=F32)
    mix_t[x, y, z] = total.astype(BF16)
    greet(me, z)

    over = push(mix_t.at[x, y, z], mix_t.at[x, y, z], xs, xr, {"mp_0": 1 - x})
    over.start()

    def task_push(o):
        return push(tt.at[me], tt.at[me], ts.at[o], tr.at[o], plane_device(lax.rem(me + o, PLANE)))

    def task_start(o, carry):
        task_push(o).start()
        return carry

    lax.fori_loop(1, PLANE, task_start, 0)
    push(mix_t.at[1 - x, y, z], mix_t.at[1 - x, y, z], xs, xr, {"mp_0": 1 - x}).wait_recv()
    z_pushes = [
        push(mix_t.at[:, y, z], mix_t.at[:, y, z], zs.at[o], zr.at[o], {"mp_2": lax.rem(z + o, 8)}) for o in range(1, 8)
    ]
    for one in z_pushes:
        one.start()
    for o in range(1, 8):
        source = lax.rem(z - o + 8, 8)
        push(mix_t.at[:, y, source], mix_t.at[:, y, source], zs.at[o], zr.at[o], {"mp_2": source}).wait_recv()
    up, down = lax.rem(y + 1, 4), lax.rem(y + 3, 4)
    y_pushes = [
        push(mix_t.at[:, y], mix_t.at[:, y], ys.at[0], yr.at[0], {"mp_1": up}),
        push(mix_t.at[:, y], mix_t.at[:, y], ys.at[1], yr.at[1], {"mp_1": down}),
    ]
    for one in y_pushes:
        one.start()
    loads[1].wait()
    loads[2].wait()

    def project(at, total):
        for half in range(2):
            columns = pl.ds(pl.multiple_of(half * 2048 + at * 512, 512), 512)
            total += jnp.dot(w[:, columns], mix_t[half, at].reshape(512, 128), preferred_element_type=F32)
        return total

    total = project(y, jnp.zeros((128, 128), F32))
    push(mix_t.at[:, down], mix_t.at[:, down], ys.at[0], yr.at[0], {"mp_1": down}).wait_recv()
    onward = push(mix_t.at[0, down], mix_t.at[0, down], ys.at[2], yr.at[2], {"mp_1": up})
    onward.start()
    push(mix_t.at[:, up], mix_t.at[:, up], ys.at[1], yr.at[1], {"mp_1": up}).wait_recv()
    back = push(mix_t.at[1, up], mix_t.at[1, up], ys.at[3], yr.at[3], {"mp_1": down})
    back.start()
    total = project(up, project(down, total))
    across = lax.rem(y + 2, 4)
    push(mix_t.at[0, across], mix_t.at[0, across], ys.at[2], yr.at[2], {"mp_1": down}).wait_recv()
    push(mix_t.at[1, across], mix_t.at[1, across], ys.at[3], yr.at[3], {"mp_1": up}).wait_recv()
    total = project(across, total)

    tb[z] = total.astype(BF16)
    u_pushes = [push(tb.at[z], tb.at[z], us.at[o], ur.at[o], {"mp_2": lax.rem(z + o, 8)}) for o in range(1, 8)]
    for one in u_pushes:
        one.start()

    def task_wait(o, carry):
        source = lax.rem(me - o + PLANE, PLANE)
        push(tt.at[source], tt.at[source], ts.at[o], tr.at[o], plane_device(source)).wait_recv()
        return carry

    lax.fori_loop(1, PLANE, task_wait, 0)
    lane = lax.broadcasted_iota(jnp.int32, (ROWS, 128), 1)
    prompt_row = lax.broadcasted_iota(jnp.int32, (ROWS, 128), 0)
    lane_task = (lane % NTASK).astype(F32)

    def select(p, carry):
        task = jnp.concatenate([tt[p], tt[p]], axis=0)
        hit = jnp.where((lane // NTASK == prompt_row) & (task == lane_task), 1.0, 0.0)
        sel[pl.ds(pl.multiple_of(p * ROWS, ROWS), ROWS), :] = hit.astype(BF16)
        return carry

    lax.fori_loop(0, PLANE, select, 0)
    for o in range(1, 8):
        source = lax.rem(z - o + 8, 8)
        push(tb.at[source], tb.at[source], us.at[o], ur.at[o], {"mp_2": source}).wait_recv()
    for i in range(4):
        for kv in range(2):
            part = slice(kv * COLS, (kv + 1) * COLS)
            head = jnp.concatenate([tb[2 * i, part, :], tb[2 * i + 1, part, :]], axis=0)
            picked = lax.dot_general(sel[...], head, (((1,), (1,)), ((), ())), preferred_element_type=F32)
            out[:, i, kv] = picked.astype(BF16).reshape(PLANE, ROWS, DH)

    heads, rows = block_of(me)
    own = pltpu.make_async_copy(out.at[me], pp.at[heads, :, rows, :], own_sem)
    own.start()

    def pair_push(o):
        p = lax.rem(me + o, PLANE)
        return push(out.at[p], pp.at[heads, :, rows, :], ps.at[o], pr.at[o], plane_device(p))

    def pair_start(o, carry):
        pair_push(o).start()
        return carry

    lax.fori_loop(1, PLANE, pair_start, 0)

    def pair_wait(o, carry):
        source = lax.rem(me - o + PLANE, PLANE)
        source_heads, source_rows = block_of(source)
        landing = pp.at[source_heads, :, source_rows, :]
        push(out.at[source], landing, ps.at[o], pr.at[o], plane_device(source)).wait_recv()
        return carry

    lax.fori_loop(1, PLANE, pair_wait, 0)
    own.wait()

    def sent_wait(o, carry):
        pair_push(o).wait_send()
        task_push(o).wait_send()
        return carry

    lax.fori_loop(1, PLANE, sent_wait, 0)
    for one in [over, onward, back, *z_pushes, *y_pushes, *u_pushes]:
        one.wait_send()


def forward(task_ids, task_logits, sp, kw, vw):
    any_space = pl.BlockSpec(memory_space=pl.ANY)
    vmem = pl.BlockSpec(memory_space=pltpu.VMEM)
    dma = pltpu.SemaphoreType.DMA
    return pl.pallas_call(
        forward_kernel,
        out_shape=(
            jax.ShapeDtypeStruct((HEADS, 2, PTOK, DH), BF16),
            jax.ShapeDtypeStruct((PLANE * ROWS, 128), BF16),
        ),
        in_specs=[pl.BlockSpec(memory_space=pltpu.SMEM), vmem, any_space, any_space, any_space],
        out_specs=(any_space, vmem),
        scratch_shapes=[
            pltpu.VMEM((2, 4, 8, COLS, 128), BF16),
            pltpu.VMEM((ROWS, COLS, NSRC), BF16),
            pltpu.VMEM((2 * COLS, D), BF16),
            pltpu.VMEM((8, 128, 128), BF16),
            pltpu.VMEM((PLANE, 8, 128), F32),
            pltpu.VMEM((PLANE, 4, 2, ROWS, DH), BF16),
            dma((3,)), dma, dma, dma, dma((8,)), dma((8,)), dma((4,)), dma((4,)), dma((8,)), dma((8,)),
            dma((PLANE,)), dma((PLANE,)), dma((PLANE,)), dma((PLANE,)),
        ],
        compiler_params=pltpu.CompilerParams(collective_id=0, has_side_effects=True),
        name="prompt_forward",
    )(task_ids, task_logits, sp, kw, vw)


HEADS_STEP = 4


def attention_kernel(q_ref, k_ref, v_ref, c_ref, pp_ref, o_ref, g_ref):
    scale = DH ** (-0.5)
    nt = (((1,), (1,)), ((), ()))
    tn = (((0,), (0,)), ((), ()))
    column = lax.broadcasted_iota(jnp.int32, (SEQ, SEQ), 1)
    position = lax.broadcasted_iota(jnp.int32, (SEQ, SEQ), 0)
    visible = column <= position
    for h in range(HEADS_STEP):
        lanes = slice(h * DH, (h + 1) * DH)
        q, k, v, cot = q_ref[:, lanes], k_ref[:, lanes], v_ref[:, lanes], c_ref[:, lanes]
        pk, pv = pp_ref[h, 0], pp_ref[h, 1]
        ps = lax.dot_general(q, pk, nt, preferred_element_type=F32) * scale
        ss = lax.dot_general(q, k, nt, preferred_element_type=F32) * scale
        ss = jnp.where(visible, ss, -1e30)
        top = jnp.maximum(jnp.max(ps, axis=1, keepdims=True), jnp.max(ss, axis=1, keepdims=True))
        pe, se = jnp.exp(ps - top), jnp.exp(ss - top)
        inverse = 1.0 / (jnp.sum(pe, axis=1, keepdims=True) + jnp.sum(se, axis=1, keepdims=True))
        pa, sa = pe * inverse, se * inverse
        par, sar = pa.astype(BF16), sa.astype(BF16)
        attended = jnp.dot(par, pv, preferred_element_type=F32) + jnp.dot(sar, v, preferred_element_type=F32)
        o_ref[:, lanes] = attended.astype(BF16)
        pg = lax.dot_general(cot, pv, nt, preferred_element_type=F32)
        sg = lax.dot_general(cot, v, nt, preferred_element_type=F32)
        inner = jnp.sum(pa * pg, axis=1, keepdims=True) + jnp.sum(sa * sg, axis=1, keepdims=True)
        gs = (pa * (pg - inner)).astype(BF16)
        g_ref[h, 0] = (lax.dot_general(gs, q, tn, preferred_element_type=F32) * scale).astype(BF16)
        g_ref[h, 1] = lax.dot_general(par, cot, tn, preferred_element_type=F32).astype(BF16)


def attention(q, k, v, cot, pp):
    wide = pl.BlockSpec((SEQ, HEADS_STEP * DH), lambda i: (0, i))
    pair = pl.BlockSpec((HEADS_STEP, 2, PTOK, DH), lambda i: (i, 0, 0, 0))
    return pl.pallas_call(
        attention_kernel,
        grid=(HEADS // HEADS_STEP,),
        out_shape=(
            jax.ShapeDtypeStruct((SEQ, D), BF16),
            jax.ShapeDtypeStruct((HEADS, 2, PTOK, DH), BF16),
        ),
        in_specs=[wide, wide, wide, wide, pair],
        out_specs=(wide, pair),
        name="prompt_attention",
    )(q, k, v, cot, pp)


def backward_kernel(
    logits, sel, sp, kw, vw, gg, source_grad, logits_grad,
    spv, w, rg, gz, rz, rt, ry, t2, rz2, sx, rx, wslot, wz,
    load_sem, own_sem, ps, pr, us, ur, ys, yr, zs, zr, xs, xr, ws, wr, vs, vr,
):
    a, c, x, y, z = here()
    d = a * 2 + c
    me = plane_index(a, c, x, y)
    tn = (((0,), (0,)), ((), ()))
    loads = (
        pltpu.make_async_copy(sp.at[pl.ds(d * ROWS, ROWS)], spv, load_sem.at[0]),
        pltpu.make_async_copy(kw, w.at[pl.ds(0, COLS)], load_sem.at[1]),
        pltpu.make_async_copy(vw, w.at[pl.ds(COLS, COLS)], load_sem.at[2]),
    )
    for load in loads:
        load.start()
    heads, rows = block_of(me)
    own = pltpu.make_async_copy(gg.at[heads, :, rows, :], rg.at[me], own_sem)
    own.start()
    greet(me, z)

    def pair_push(o):
        p = lax.rem(me + o, PLANE)
        p_heads, p_rows = block_of(p)
        return push(gg.at[p_heads, :, p_rows, :], rg.at[me], ps.at[o], pr.at[o], plane_device(p))

    def pair_start(o, carry):
        pair_push(o).start()
        return carry

    lax.fori_loop(1, PLANE, pair_start, 0)

    def pair_wait(o, carry):
        source = lax.rem(me - o + PLANE, PLANE)
        push(gg.at[heads, :, rows, :], rg.at[source], ps.at[o], pr.at[o], plane_device(source)).wait_recv()
        return carry

    lax.fori_loop(1, PLANE, pair_wait, 0)
    own.wait()
    for i in range(4):
        for kv in range(2):
            arrived = rg[:, i, kv].reshape(PLANE * ROWS, DH)
            summed = lax.dot_general(arrived, sel[...], tn, preferred_element_type=F32).astype(BF16)
            gz[2 * i, kv * COLS : (kv + 1) * COLS, :] = summed[:COLS]
            gz[2 * i + 1, kv * COLS : (kv + 1) * COLS, :] = summed[COLS:]

    u_pushes = []
    for o in range(1, 8):
        other = lax.rem(z + o, 8)
        u_pushes.append(push(gz.at[other], rz.at[o], us.at[o], ur.at[o], {"mp_2": other}))
    for one in u_pushes:
        one.start()
    loads[1].wait()
    loads[2].wait()
    grad = gz[z].astype(F32)
    for o in range(1, 8):
        push(gz.at[z], rz.at[o], us.at[o], ur.at[o], {"mp_2": lax.rem(z - o + 8, 8)}).wait_recv()
        grad += rz[o].astype(F32)
    grad_high = grad.astype(BF16)
    grad_low = (grad - grad_high.astype(F32)).astype(BF16)

    def row_terms(at):
        for half in range(2):
            columns = pl.ds(pl.multiple_of(half * 2048 + at * 512, 512), 512)
            part = w[:, columns]
            terms = lax.dot_general(part, grad_high, tn, preferred_element_type=F32)
            terms += lax.dot_general(part, grad_low, tn, preferred_element_type=F32)
            rt[at, half] = terms.astype(BF16).reshape(8, COLS, 128)

    y_pushes = []
    for o in (2, 1, 3):
        other = lax.rem(y + o, 4)
        row_terms(other)
        one = push(rt.at[other], ry.at[o], ys.at[o], yr.at[o], {"mp_1": other})
        one.start()
        y_pushes.append(one)
    row_terms(y)
    for o in range(1, 4):
        push(rt.at[y], ry.at[o], ys.at[o], yr.at[o], {"mp_1": lax.rem(y - o + 4, 4)}).wait_recv()
    for half in range(2):
        four = rt[y, half].astype(F32)
        for o in range(1, 4):
            four += ry[o, half].astype(F32)
        t2[:, half] = four.astype(BF16)
    z_pushes = []
    for o in range(1, 8):
        other = lax.rem(z + o, 8)
        one = push(t2.at[other], rz2.at[o], zs.at[o], zr.at[o], {"mp_2": other})
        one.start()
        z_pushes.append(one)
    eight = t2[z].astype(F32)
    for o in range(1, 8):
        push(t2.at[z], rz2.at[o], zs.at[o], zr.at[o], {"mp_2": lax.rem(z - o + 8, 8)}).wait_recv()
        eight += rz2[o].astype(F32)
    sx[...] = eight
    over = push(sx.at[1 - x], rx, xs, xr, {"mp_0": 1 - x})
    over.start()
    mix = soft(logits[...])
    loads[0].wait()
    push(sx.at[1 - x], rx, xs, xr, {"mp_0": 1 - x}).wait_recv()
    mixture_grad = sx[x] + rx[...]

    flipped = mixture_grad.T
    part = jnp.zeros((NTASK, NSRC), F32)
    for r in range(ROWS):
        part += jnp.dot(
            flipped[r * NTASK : (r + 1) * NTASK], spv[r].astype(F32), precision=HIGH, preferred_element_type=F32
        )
    wslot[me] = part

    def weight_push(o):
        return push(wslot.at[me], wslot.at[me], ws.at[o], wr.at[o], plane_device(lax.rem(me + o, PLANE)))

    def weight_start(o, carry):
        weight_push(o).start()
        return carry

    lax.fori_loop(1, PLANE, weight_start, 0)
    tile = jnp.concatenate([mix] * ROWS, axis=0)
    lane = lax.broadcasted_iota(jnp.int32, (COLS, 128), 1)
    for r in range(ROWS):
        chosen = jnp.where(lane // NTASK == r, mixture_grad, 0.0)
        source_grad[r] = jnp.dot(chosen, tile, precision=HIGH, preferred_element_type=F32)

    def weight_wait(o, carry):
        source = lax.rem(me - o + PLANE, PLANE)
        push(wslot.at[source], wslot.at[source], ws.at[o], wr.at[o], plane_device(source)).wait_recv()
        return carry

    lax.fori_loop(1, PLANE, weight_wait, 0)
    wz[z] = jnp.sum(wslot[...], axis=0)
    v_pushes = [push(wz.at[z], wz.at[z], vs.at[o], vr.at[o], {"mp_2": lax.rem(z + o, 8)}) for o in range(1, 8)]
    for one in v_pushes:
        one.start()
    for o in range(1, 8):
        source = lax.rem(z - o + 8, 8)
        push(wz.at[source], wz.at[source], vs.at[o], vr.at[o], {"mp_2": source}).wait_recv()
    weight_grad = jnp.sum(wz[...], axis=0)
    logits_grad[...] = mix * (weight_grad - jnp.sum(mix * weight_grad, axis=1, keepdims=True))

    def sent_wait(o, carry):
        pair_push(o).wait_send()
        weight_push(o).wait_send()
        return carry

    lax.fori_loop(1, PLANE, sent_wait, 0)
    for one in [over, *u_pushes, *y_pushes, *z_pushes, *v_pushes]:
        one.wait_send()


def backward(task_logits, sel, sp, kw, vw, gg):
    any_space = pl.BlockSpec(memory_space=pl.ANY)
    vmem = pl.BlockSpec(memory_space=pltpu.VMEM)
    dma = pltpu.SemaphoreType.DMA
    return pl.pallas_call(
        backward_kernel,
        out_shape=(
            jax.ShapeDtypeStruct((ROWS, COLS, NSRC), F32),
            jax.ShapeDtypeStruct((NTASK, NSRC), F32),
        ),
        in_specs=[vmem, vmem, any_space, any_space, any_space, any_space],
        out_specs=(vmem, vmem),
        scratch_shapes=[
            pltpu.VMEM((ROWS, COLS, NSRC), BF16),
            pltpu.VMEM((2 * COLS, D), BF16),
            pltpu.VMEM((PLANE, 4, 2, ROWS, DH), BF16),
            pltpu.VMEM((8, 128, 128), BF16),
            pltpu.VMEM((8, 128, 128), BF16),
            pltpu.VMEM((4, 2, 8, COLS, 128), BF16),
            pltpu.VMEM((4, 2, 8, COLS, 128), BF16),
            pltpu.VMEM((8, 2, COLS, 128), BF16),
            pltpu.VMEM((8, 2, COLS, 128), BF16),
            pltpu.VMEM((2, COLS, 128), F32),
            pltpu.VMEM((COLS, 128), F32),
            pltpu.VMEM((PLANE, NTASK, NSRC), F32),
            pltpu.VMEM((8, NTASK, NSRC), F32),
            dma((3,)), dma, dma((PLANE,)), dma((PLANE,)), dma((8,)), dma((8,)), dma((4,)), dma((4,)),
            dma((8,)), dma((8,)), dma, dma, dma((PLANE,)), dma((PLANE,)), dma((8,)), dma((8,)),
        ],
        compiler_params=pltpu.CompilerParams(collective_id=1, has_side_effects=True),
        name="prompt_backward",
    )(task_logits, sel, sp, kw, vw, gg)


def on_device(source_prompts, task_logits, task_ids, key_weight, value_weight, queries, keys, values, cotangent):
    sp = source_prompts.transpose(1, 2, 0)
    kw, vw = key_weight.T, value_weight.T
    pp, sel = forward(task_ids, task_logits, sp, kw, vw)
    attended, gg = attention(queries[0], keys[0], values[0], cotangent[0], pp)
    source_grad, logits_grad = backward(task_logits, sel, sp, kw, vw, gg)
    return attended[None], source_grad.transpose(2, 0, 1), logits_grad


def solution(mesh):
    torus = Mesh(mesh.devices.reshape(2, 2, 2, 4, 8), AXES)
    return jax.shard_map(
        on_device,
        mesh=torus,
        in_specs=(
            P(None, None, MP),
            P(),
            P(DP),
            P(None, MP),
            P(None, MP),
            P(AXES, None, None),
            P(AXES, None, None),
            P(AXES, None, None),
            P(AXES, None, None),
        ),
        out_specs=(P(AXES, None, None), P(None, DP, MP), P()),
        check_vma=False,
    )
```

time: 432 us -> 152 us (0.35); the launches traced: 424 us -> 151 us
  Pallas kernels: 0 us -> 148 us
  waiting for transfers between devices: 137 us -> 0 us
  local copies, waits for them, and re-layouts: 125 us -> 2.48 us
  blocking collectives: 105 us -> 0 us
  matrix products: 18.2 us -> 0 us
  starting transfers between devices: 16.1 us -> 0 us
  between operations: 14.6 us -> 0.66 us
  other arithmetic: 7.71 us -> 0 us
    pallas_call x0 -> x3, Pallas kernels: none -> 148 us  [the longest x1 68.7 us: backward(): pl.pallas_call(backward_kernel, out_shape=(jax.ShapeDtypeStruct((ROWS, CO...]
    all_gather x1 -> x0, waiting for transfers between devices: 94.3 us -> none  [all_blocks(): blocks = lax.all_gather(blocks, axes[k], axis=0, tiled=True)]
    all_to_all x2 -> x0, blocking collectives: 43.7 us -> none  [the longest x1 33.9 us: on_device(): lax.all_to_all(outgoing_grads, MP, split_axis=3, concat_axis=0, tiled=True)]
    all_to_all x2 -> x0, waiting for transfers between devices: 43.1 us -> none  [the longest x1 22.6 us: sum_at_owner(): lax.all_to_all(blocks, axis, split_axis=0, concat_axis=0, tiled=True)]
    psum x5 -> x0, blocking collectives: 39.3 us -> none  [one_axis_at_a_time(): array = lax.psum(array, axis)]
    unnamed x44 -> x4, local copies, waits for them, and re-layouts: 40.8 us -> 2.48 us
    transpose x2 -> x0, local copies, waits for them, and re-layouts: 22.3 us -> none  [the longest x1 12 us: in_order(): blocks = jnp.moveaxis(blocks, 0, dim)]
    all_gather x2 -> x0, blocking collectives: 22 us -> none  [all_blocks(): blocks = lax.all_gather(blocks, axes[k], axis=0, tiled=True)]
  transfers between devices with their start and end apart: 3 -> 0, of which waited for: 3 -> 0; matrix products, arithmetic and copies ran while one was open for 4% -> 0% of each run, Pallas kernels for 0% -> 0%
where the time goes in v1:
time: 152 us; the launch traced here: 151 us
  Pallas kernels  148 us (97%)
  local copies, waits for them, and re-layouts  2.48 us (2%)
    pallas_call x1, Pallas kernels, backward(): pl.pallas_call(backward_kernel, out_shape=(jax.ShapeDtypeStruct((ROWS, CO...  68.7 us
    pallas_call x1, Pallas kernels, forward(): pl.pallas_call(forward_kernel, out_shape=(jax.ShapeDtypeStruct((HEADS, 2,...  54.9 us
    pallas_call x1, Pallas kernels, attention(): pl.pallas_call(attention_kernel, grid=(HEADS // HEADS_STEP,), out_shape=(...  24.1 us

profile of v1, /device:TPU:8, one launch (start us, length us, event | category | flops | bytes accessed | tf_op | source)
XLA Modules:
  0.0 150.8 jit_solution(17808281766064252200)
XLA Ops:
  0.6 54.9 %prompt_forward.1 = (bf16[32,2,64,128]{3,2,1,0:T(8,128)(2,1)}, bf16[512,128]{1,0:T(8,128)(2,1)}) custom-call(s32[64]{0:T(128)} %tids.1, f32[8,128]{1,0:T(8,128)} %logits.3, bf16[64,64,128]{2,1,0:T(8,128)(2,1)} %bitcast.9, bf16[64,4096]{1,0:T(8,128)(2,1)} %bitcast.11, bf16[64,4096]{1,0:T(8,128)(2,1)} %bitcast.13), custom_call_target="tpu_custom_call" | custom-call | tf_op jit(solution)/shard_map/prompt_forward/pallas_call | solution.py:220
  55.5 24.1 %prompt_attention.1 = (bf16[128,4096]{1,0:T(8,128)(2,1)}, bf16[32,2,64,128]{3,2,1,0:T(8,128)(2,1)}) custom-call(bf16[128,4096]{1,0:T(8,128)(2,1)} %bitcast.15, bf16[128,4096]{1,0:T(8,128)(2,1)} %bitcast.16, bf16[128,4096]{1,0:T(8,128)(2,1)} %bitcast.17, bf16[128,4096]{1,0:T(8,128)(2,1)} %bitcast.18, bf16[32,2,64,128]{3,2,1,0:T(8,128)(2,1)} %get-tuple-element.9.pp_ref), custom_call_target="tpu_custom_call" | custom-call | tf_op jit(solution)/shard_map/prompt_attention/pallas_call | solution.py:278
  79.6 68.7 %prompt_backward.1 = (f32[16,64,128]{2,1,0:T(8,128)}, f32[8,128]{1,0:T(8,128)}) custom-call(f32[8,128]{1,0:T(8,128)} %logits.3, bf16[512,128]{1,0:T(8,128)(2,1)} %get-tuple-element.11.sel, bf16[64,64,128]{2,1,0:T(8,128)(2,1)} %bitcast.10, bf16[64,4096]{1,0:T(8,128)(2,1)} %bitcast.12, bf16[64,4096]{1,0:T(8,128)(2,1)} %bitcast.14, ...), custom_call_target="tpu_custom_call" | custom-call | tf_op jit(solution)/shard_map/prompt_backward/pallas_call | solution.py:445
  148.3 0.0 copy-start
  148.4 1.9 %copy.14 = f32[128,16,64]{0,2,1:T(8,128)} copy(f32[128,16,64]{0,2,1:T(8,128)} %bitcast.19) | data formatting | bytes 1048576
  150.2 0.0 copy-done
  150.2 0.6 copy.15
Async XLA Ops:
  148.3 1.9 %copy-start = (f32[8,128]{1,0:T(8,128)S(1)}, f32[8,128]{1,0:T(8,128)}, u32[]{:S(2)}) copy-start(f32[8,128]{1,0:T(8,128)} %get-tuple-element.20) | copy-start | bytes 12292

commit v2 on v0

v2 whole, which is shorter than its diff:
```python
import functools

import jax
import jax.numpy as jnp
from jax import lax
from jax.experimental import pallas as pl
from jax.experimental.pallas import tpu as pltpu
from jax.sharding import Mesh
from jax.sharding import PartitionSpec as P

D = 4096
HEADS = 32
DH = 128
NSRC = 128
NTASK = 8
PTOK = 64
SEQ = 128
AXES = ("dp_0", "dp_1", "mp_0", "mp_1", "mp_2")
MP = ("mp_0", "mp_1", "mp_2")
DP = ("dp_0", "dp_1")
MESH = pl.DeviceIdType.MESH
ROWS = 16
COLS = 64
PLANE = 32
F32 = jnp.float32
BF16 = jnp.bfloat16
HIGH = lax.Precision.HIGHEST


def here():
    return tuple(lax.axis_index(name) for name in AXES)


def push(src, dst, sent, landed, device):
    return pltpu.make_async_remote_copy(
        src_ref=src, dst_ref=dst, send_sem=sent, recv_sem=landed, device_id=device, device_id_type=MESH
    )


def soft(logits):
    exponent = jnp.exp(logits - jnp.max(logits, axis=1, keepdims=True))
    return exponent / jnp.sum(exponent, axis=1, keepdims=True)


NN = (((1,), (0,)), ((), ()))
NT = (((1,), (1,)), ((), ()))
TN = (((0,), (0,)), ((), ()))
SCALE = DH ** (-0.5)
HOPS = (0, 1, 3, 2)
PRE_HEADS = 2
MID_HEADS = 2
POST_HEADS = 2


def dot(a, b, dims=NN):
    return lax.dot_general(a, b, dims, preferred_element_type=F32)


def kernel(
    tids, logits, sp, kw, vw, queries, keys, values, cotangent,
    attended, source_grad, logits_grad,
    spv, w, qv, kv, vv, cv, mix_t, tb, tt, sel, out, pp, stat, self_e, pat, gg, rg, gz, rz, rt, ry, t2, rz2, sx, rx,
    wslot, wz,
    load_sem, zs, zr, xs, xr, ys, yr, us, ur, ts, tr, ps, pr, gs, gr, bs, br, cs, cr, es, er, fs, fr, ws, wr, vs, vr,
):
    a, c, x, y, z = here()
    d, g = a * 2 + c, x * 4 + y
    me = d * 8 + g
    pair = lax.div(z, 2)
    barrier = pltpu.get_barrier_semaphore()

    def device(d_to, g_to):
        return {
            "dp_0": lax.div(d_to, 2), "dp_1": lax.rem(d_to, 2), "mp_0": lax.div(g_to, 4), "mp_1": lax.rem(g_to, 4),
        }

    def along(o, n, at):
        return lax.rem(at + o + n, n)

    def around(m):
        k, dd = lax.div(m, 4), lax.rem(m, 4)
        return along(dd, 4, d), along(-k, 8, g), along(-dd, 4, d), along(k, 8, g)

    def plane(body):
        lax.fori_loop(1, PLANE, lambda m, carry: (body(m), carry)[1], 0)

    def rows(quarter):
        return pl.ds(pl.multiple_of(quarter * ROWS, ROWS), ROWS)

    def signal(m):
        d_to, g_to, _, _ = around(m)
        pl.semaphore_signal(barrier, inc=1, device_id=device(d_to, g_to), device_id_type=MESH)

    plane(signal)
    for o in range(1, 8):
        pl.semaphore_signal(barrier, inc=1, device_id={"mp_2": along(o, 8, z)}, device_id_type=MESH)
    loads = [
        pltpu.make_async_copy(sp.at[pl.ds(d * ROWS, ROWS)], spv, load_sem.at[0]),
        pltpu.make_async_copy(queries, qv, load_sem.at[1]),
        pltpu.make_async_copy(keys, kv, load_sem.at[2]),
        pltpu.make_async_copy(cotangent, cv, load_sem.at[3]),
        pltpu.make_async_copy(values, vv, load_sem.at[4]),
        pltpu.make_async_copy(kw, w.at[pl.ds(0, COLS)], load_sem.at[5]),
        pltpu.make_async_copy(vw, w.at[pl.ds(COLS, COLS)], load_sem.at[6]),
    ]
    for load in loads:
        load.start()
    tt[me] = jnp.full((8, 128), tids[x * 32 + y * 8 + z], jnp.int32).astype(F32)
    tile = jnp.concatenate([soft(logits[...]).astype(BF16).astype(F32)] * ROWS, axis=0)
    row = lax.broadcasted_iota(jnp.int32, (128, 128), 0)
    loads[0].wait()
    total = jnp.zeros((COLS, 128), F32)
    for r in range(ROWS):
        weights = jnp.where(row // NTASK == r, tile, 0.0).astype(BF16)
        total += dot(spv[r], weights, NT)
    mix_t[x, y, z] = total.astype(BF16)
    pl.semaphore_wait(barrier, PLANE - 1 + 7)

    sends = []

    def send(src, dst, sent, landed, to):
        one = push(src, dst, sent, landed, to)
        one.start()
        sends.append(one)

    own = mix_t.at[x, y, z]
    for o in (1, 7, 2, 6, 3, 5, 4):
        send(own, own, zs.at[o], zr.at[o], {"mp_2": along(o, 8, z)})

    def task_push(m):
        d_to, g_to, d_from, g_from = around(m)
        return push(tt.at[me], tt.at[me], ts.at[m], tr.at[m], device(d_to, g_to))

    plane(lambda m: task_push(m).start())

    def pre(first, count):
        masked = lax.broadcasted_iota(jnp.int32, (SEQ, SEQ), 0) > lax.broadcasted_iota(jnp.int32, (SEQ, SEQ), 1)

        def step(n, carry):
            for e in range(PRE_HEADS):
                h = first + n * PRE_HEADS + e
                lanes = pl.ds(pl.multiple_of(h * DH, DH), DH)
                scores = dot(kv[:, lanes], qv[:, lanes], NT) * SCALE
                scores = jnp.where(masked, -1e30, scores)
                top = jnp.max(scores, axis=0, keepdims=True)
                exponent = jnp.exp(scores - top)
                grad = dot(vv[:, lanes], cv[:, lanes], NT)
                self_e[h] = exponent
                stat[h, 0:1] = top
                stat[h, 1:2] = jnp.sum(exponent, axis=0, keepdims=True)
                stat[h, 2:3] = jnp.sum(exponent * grad, axis=0, keepdims=True)
            return carry

        lax.fori_loop(0, count // PRE_HEADS, step, 0)

    for load in loads[1:5]:
        load.wait()
    pre(0, 10)
    for o in (1, 7, 2, 6, 3, 5, 4):
        source = along(-o, 8, z)
        push(mix_t.at[x, y, source], mix_t.at[x, y, source], zs.at[o], zr.at[o], {"mp_2": source}).wait_recv()
    up, down, across = along(1, 4, y), along(-1, 4, y), along(2, 4, y)
    other = 1 - x

    def y_start(half, n):
        block = mix_t.at[half, y]
        send(block, block, ys.at[n, 0], yr.at[n, 0], {"mp_1": up})
        send(block, block, ys.at[n, 1], yr.at[n, 1], {"mp_1": down})

    def y_relay(half, n):
        block, part = mix_t.at[half, down], mix_t.at[half, down, pl.ds(0, 4)]
        push(block, block, ys.at[n, 0], yr.at[n, 0], {"mp_1": down}).wait_recv()
        send(part, part, ys.at[n, 2], yr.at[n, 2], {"mp_1": up})
        block, part = mix_t.at[half, up], mix_t.at[half, up, pl.ds(4, 4)]
        push(block, block, ys.at[n, 1], yr.at[n, 1], {"mp_1": up}).wait_recv()
        send(part, part, ys.at[n, 3], yr.at[n, 3], {"mp_1": down})

    def y_end(half, n):
        part = mix_t.at[half, across, pl.ds(0, 4)]
        push(part, part, ys.at[n, 2], yr.at[n, 2], {"mp_1": down}).wait_recv()
        part = mix_t.at[half, across, pl.ds(4, 4)]
        push(part, part, ys.at[n, 3], yr.at[n, 3], {"mp_1": up}).wait_recv()

    def project(half, at):
        columns = pl.ds(pl.multiple_of(half * 2048 + at * 512, 512), 512)
        return dot(w[:, columns], mix_t[half, at].reshape(512, 128))

    y_start(x, 0)
    send(mix_t.at[x, y], mix_t.at[x, y], xs, xr, {"mp_0": other})
    for load in loads[5:]:
        load.wait()
    pre(10, 8)
    total = project(x, y)
    push(mix_t.at[other, y], mix_t.at[other, y], xs, xr, {"mp_0": other}).wait_recv()
    y_start(other, 1)
    y_relay(x, 0)
    total += project(other, y) + project(x, down) + project(x, up)

    def task_wait(m):
        d_to, g_to, d_from, g_from = around(m)
        slot = tt.at[d_from * 8 + g_from]
        push(slot, slot, ts.at[m], tr.at[m], device(d_from, g_from)).wait_recv()

    plane(task_wait)
    lane = lax.broadcasted_iota(jnp.int32, (ROWS, 128), 1)
    prompt_row = lax.broadcasted_iota(jnp.int32, (ROWS, 128), 0)
    lane_task = (lane % NTASK).astype(F32)

    def select(p, carry):
        task = jnp.concatenate([tt[p], tt[p]], axis=0)
        hit = jnp.where((lane // NTASK == prompt_row) & (task == lane_task), 1.0, 0.0)
        sel[rows(p), :] = hit.astype(BF16)
        return carry

    lax.fori_loop(0, PLANE, select, 0)
    y_relay(other, 1)
    y_end(x, 0)
    total += project(other, down) + project(other, up) + project(x, across)
    y_end(other, 1)
    total += project(other, across)

    tb[z] = total.astype(BF16)
    mate = pair * 2 + 1 - lax.rem(z, 2)

    def u_send(to):
        o = along(to - z, 8, 0)
        send(tb.at[z], tb.at[z], us.at[o], ur.at[o], {"mp_2": to})

    def u_wait(source):
        o = along(z - source, 8, 0)
        push(tb.at[source], tb.at[source], us.at[o], ur.at[o], {"mp_2": source}).wait_recv()

    u_send(mate)
    for hop in HOPS[1:]:
        for side in range(2):
            u_send(along(-hop, 4, pair) * 2 + side)

    def pair_push(j, i, m):
        d_to, g_to, d_from, g_from = around(m)
        return push(
            out.at[i, d_to * 8 + g_to], pp.at[i, g, :, rows(d), :], ps.at[j, m], pr.at[j, m], device(d_to, g_to)
        )

    pieces = [along(hop, 4, pair) for hop in HOPS]
    for j, i in enumerate(pieces):
        if j == 0:
            pre(18, 4)
            u_wait(mate)
        else:
            u_wait(2 * i)
            u_wait(2 * i + 1)
        for which in range(2):
            part = slice(which * COLS, (which + 1) * COLS)
            table = jnp.concatenate([tb[2 * i, part, :], tb[2 * i + 1, part, :]], axis=0)
            out[i, :, which] = dot(sel[...], table, NT).astype(BF16).reshape(PLANE, ROWS, DH)
        plane(functools.partial(lambda j, i, m: pair_push(j, i, m).start(), j, i))
        for which in range(2):
            pp[i, g, which, rows(d), :] = out[i, me, which]
    pre(22, 10)

    def mid(j, i, k, skip_own):
        g_here = along(k, 8, g)
        for dd in range(1 if skip_own else 0, 4):
            d_from = along(-dd, 4, d)
            landing = pp.at[i, g_here, :, rows(d_from), :]
            m = k * 4 + dd
            push(landing, landing, ps.at[j, m], pr.at[j, m], device(d_from, g_here)).wait_recv()
        return g_here

    def head(i, g_here):
        h = g_here * 4 + i
        lanes = pl.ds(pl.multiple_of(h * DH, DH), DH)
        q, cot = qv[:, lanes], cv[:, lanes]
        scores = dot(pp[i, g_here, 0], q, NT) * SCALE
        grad = dot(pp[i, g_here, 1], cot, NT)
        self_top = stat[h, 0:1]
        top = jnp.maximum(jnp.max(scores, axis=0, keepdims=True), self_top)
        exponent = jnp.exp(scores - top)
        shrink = jnp.exp(self_top - top)
        inverse = 1.0 / (shrink * stat[h, 1:2] + jnp.sum(exponent, axis=0, keepdims=True))
        attention = exponent * inverse
        self_scale = shrink * inverse
        stat[h, 3:4] = self_scale
        rounded = attention.astype(BF16)
        pat[h] = rounded
        inner = self_scale * stat[h, 2:3] + jnp.sum(attention * grad, axis=0, keepdims=True)
        grad_scores = (attention * (grad - inner)).astype(BF16)
        gg[i, g_here, 0] = (dot(grad_scores, q) * SCALE).astype(BF16)
        gg[i, g_here, 1] = dot(rounded, cot).astype(BF16)

    def grad_push(j, i, k, dd):
        m = k * 4 + dd
        d_to, g_here = along(dd, 4, d), along(k, 8, g)
        return push(
            gg.at[i, g_here, :, rows(d_to), :], rg.at[i, me], gs.at[j, m], gr.at[j, m], device(d_to, g_here)
        )

    def mid_step(j, i, ks, skip_own):
        groups = [mid(j, i, k, skip_own and n == 0) for n, k in enumerate(ks)]
        for g_here in groups:
            head(i, g_here)
        for n, k in enumerate(ks):
            for dd in range(1 if skip_own and n == 0 else 0, 4):
                grad_push(j, i, k, dd).start()

    for j, i in enumerate(pieces):
        mid_step(j, i, list(range(MID_HEADS)), True)
        rg[i, me] = gg[i, g, :, rows(d), :]

        def later(n, carry, j=j, i=i):
            mid_step(j, i, [n * MID_HEADS + e for e in range(MID_HEADS)], False)
            return carry

        lax.fori_loop(1, 8 // MID_HEADS, later, 0)

    def post(first, count):
        def step(n, carry):
            for e in range(POST_HEADS):
                h = first + n * POST_HEADS + e
                lanes = pl.ds(pl.multiple_of(h * DH, DH), DH)
                self_part = (self_e[h] * stat[h, 3:4]).astype(BF16)
                prompt_values = pp[lax.rem(h, 4), lax.div(h, 4), 1]
                summed = dot(self_part, vv[:, lanes], TN) + dot(pat[h], prompt_values, TN)
                attended[:, lanes] = summed.astype(BF16)
            return carry

        lax.fori_loop(0, count // POST_HEADS, step, 0)

    post(0, 8)

    for j, i in enumerate(pieces):

        def grad_wait(m, j=j, i=i):
            k, dd = lax.div(m, 4), lax.rem(m, 4)
            d_from, g_from = along(-dd, 4, d), along(-k, 8, g)
            landing = rg.at[i, d_from * 8 + g_from]
            push(landing, landing, gs.at[j, m], gr.at[j, m], device(d_from, g_from)).wait_recv()

        plane(grad_wait)
        for which in range(2):
            summed = dot(rg[i, :, which].reshape(PLANE * ROWS, DH), sel[...], TN).astype(BF16)
            part = slice(which * COLS, (which + 1) * COLS)
            gz[2 * i, part, :] = summed[:COLS]
            gz[2 * i + 1, part, :] = summed[COLS:]
        for to in (mate,) if j == 0 else (2 * i, 2 * i + 1):
            o = along(to - z, 8, 0)
            send(gz.at[to], rz.at[o], bs.at[o], br.at[o], {"mp_2": to})
    post(8, 8)
    grad = gz[z].astype(F32)
    for o in (1, 7, 2, 6, 3, 5, 4):
        push(gz.at[z], rz.at[o], bs.at[o], br.at[o], {"mp_2": along(-o, 8, z)}).wait_recv()
        grad += rz[o].astype(F32)
    grad_high = grad.astype(BF16)
    grad_low = (grad - grad_high.astype(F32)).astype(BF16)
    grad_both = jnp.concatenate([grad_high, grad_low], axis=1)

    def row_terms(half, at):
        columns = pl.ds(pl.multiple_of(half * 2048 + at * 512, 512), 512)
        terms = dot(w[:, columns], grad_both, TN)
        rt[half, at] = (terms[:, :128] + terms[:, 128:]).astype(BF16).reshape(8, COLS, 128)

    halves = (other, x)
    for n, half in enumerate(halves):
        for o in (2, 1, 3):
            to = along(o, 4, y)
            row_terms(half, to)
            send(rt.at[half, to], ry.at[n, o], cs.at[n, o], cr.at[n, o], {"mp_1": to})
        row_terms(half, y)

    def y_sum(n, half):
        four = rt[half, y].astype(F32)
        for o in (1, 3, 2):
            push(rt.at[half, y], ry.at[n, o], cs.at[n, o], cr.at[n, o], {"mp_1": along(-o, 4, y)}).wait_recv()
            four += ry[n, o].astype(F32)
        t2[n] = four.astype(BF16)
        for o in (1, 7, 2, 6, 3, 5, 4):
            to = along(o, 8, z)
            send(t2.at[n, to], rz2.at[n, o], es.at[n, o], er.at[n, o], {"mp_2": to})

    def z_sum(n):
        eight = t2[n, z].astype(F32)
        for o in (1, 7, 2, 6, 3, 5, 4):
            push(t2.at[n, z], rz2.at[n, o], es.at[n, o], er.at[n, o], {"mp_2": along(-o, 8, z)}).wait_recv()
            eight += rz2[n, o].astype(F32)
        return eight

    post(16, 12)
    y_sum(0, other)
    y_sum(1, x)
    sx[...] = z_sum(0)
    send(sx, rx, fs, fr, {"mp_0": other})
    post(28, 4)
    mix = soft(logits[...])
    mine = z_sum(1)
    push(sx, rx, fs, fr, {"mp_0": other}).wait_recv()
    mixture_grad = mine + rx[...]

    flipped = mixture_grad.T
    part = jnp.zeros((NTASK, NSRC), F32)
    for r in range(ROWS):
        part += jnp.dot(
            flipped[r * NTASK : (r + 1) * NTASK], spv[r].astype(F32), precision=HIGH, preferred_element_type=F32
        )
    wslot[me] = part

    def weight_push(m):
        d_to, g_to, d_from, g_from = around(m)
        return push(wslot.at[me], wslot.at[me], ws.at[m], wr.at[m], device(d_to, g_to))

    plane(lambda m: weight_push(m).start())
    tile = jnp.concatenate([mix] * ROWS, axis=0)
    lane = lax.broadcasted_iota(jnp.int32, (COLS, 128), 1)
    for r in range(ROWS):
        chosen = jnp.where(lane // NTASK == r, mixture_grad, 0.0)
        source_grad[r] = jnp.dot(chosen, tile, precision=HIGH, preferred_element_type=F32)

    def weight_wait(m):
        d_to, g_to, d_from, g_from = around(m)
        slot = wslot.at[d_from * 8 + g_from]
        push(slot, slot, ws.at[m], wr.at[m], device(d_from, g_from)).wait_recv()

    plane(weight_wait)
    wz[z] = jnp.sum(wslot[...], axis=0)
    for o in range(1, 8):
        send(wz.at[z], wz.at[z], vs.at[o], vr.at[o], {"mp_2": along(o, 8, z)})
    for o in range(1, 8):
        source = along(-o, 8, z)
        push(wz.at[source], wz.at[source], vs.at[o], vr.at[o], {"mp_2": source}).wait_recv()
    weight_grad = jnp.sum(wz[...], axis=0)
    logits_grad[...] = mix * (weight_grad - jnp.sum(mix * weight_grad, axis=1, keepdims=True))

    def sent(m):
        task_push(m).wait_send()
        weight_push(m).wait_send()
        for j, i in enumerate(pieces):
            pair_push(j, i, m).wait_send()
            grad_push(j, i, lax.div(m, 4), lax.rem(m, 4)).wait_send()

    plane(sent)
    for one in sends:
        one.wait_send()


def on_device(source_prompts, task_logits, task_ids, key_weight, value_weight, queries, keys, values, cotangent):
    any_space = pl.BlockSpec(memory_space=pl.ANY)
    vmem = pl.BlockSpec(memory_space=pltpu.VMEM)
    dma = pltpu.SemaphoreType.DMA
    block = (2, 8, COLS, 128)
    attended, source_grad, logits_grad = pl.pallas_call(
        kernel,
        out_shape=(
            jax.ShapeDtypeStruct((SEQ, D), BF16),
            jax.ShapeDtypeStruct((ROWS, COLS, NSRC), F32),
            jax.ShapeDtypeStruct((NTASK, NSRC), F32),
        ),
        in_specs=[pl.BlockSpec(memory_space=pltpu.SMEM), vmem] + [any_space] * 7,
        out_specs=(vmem, vmem, vmem),
        scratch_shapes=[
            pltpu.VMEM((ROWS, COLS, NSRC), BF16),
            pltpu.VMEM((2 * COLS, D), BF16),
            *[pltpu.VMEM((SEQ, D), BF16)] * 4,
            pltpu.VMEM((2, 4, 8, COLS, 128), BF16),
            pltpu.VMEM((8, 128, 128), BF16),
            pltpu.VMEM((PLANE, 8, 128), F32),
            pltpu.VMEM((PLANE * ROWS, 128), BF16),
            pltpu.VMEM((4, PLANE, 2, ROWS, DH), BF16),
            pltpu.VMEM((4, 8, 2, PTOK, DH), BF16),
            pltpu.VMEM((HEADS, 8, SEQ), F32),
            pltpu.VMEM((HEADS, SEQ, SEQ), F32),
            pltpu.VMEM((HEADS, PTOK, SEQ), BF16),
            pltpu.VMEM((4, 8, 2, PTOK, DH), BF16),
            pltpu.VMEM((4, PLANE, 2, ROWS, DH), BF16),
            pltpu.VMEM((8, 128, 128), BF16),
            pltpu.VMEM((8, 128, 128), BF16),
            pltpu.VMEM((2, 4, 8, COLS, 128), BF16),
            pltpu.VMEM((2, 4, 8, COLS, 128), BF16),
            pltpu.VMEM(block, BF16),
            pltpu.VMEM(block, BF16),
            pltpu.VMEM((COLS, 128), F32),
            pltpu.VMEM((COLS, 128), F32),
            pltpu.VMEM((PLANE, NTASK, NSRC), F32),
            pltpu.VMEM((8, NTASK, NSRC), F32),
            dma((7,)), dma((8,)), dma((8,)), dma, dma, dma((2, 4)), dma((2, 4)), dma((8,)), dma((8,)),
            dma((PLANE,)), dma((PLANE,)), dma((4, PLANE)), dma((4, PLANE)), dma((4, PLANE)), dma((4, PLANE)),
            dma((8,)), dma((8,)), dma((2, 4)), dma((2, 4)), dma((2, 8)), dma((2, 8)), dma, dma,
            dma((PLANE,)), dma((PLANE,)), dma((8,)), dma((8,)),
        ],
        compiler_params=pltpu.CompilerParams(collective_id=0, has_side_effects=True),
        name="prompt_step",
    )(
        task_ids, task_logits, source_prompts.transpose(1, 2, 0), key_weight.T, value_weight.T,
        queries[0], keys[0], values[0], cotangent[0],
    )
    return attended[None], source_grad.transpose(2, 0, 1), logits_grad


def solution(mesh):
    torus = Mesh(mesh.devices.reshape(2, 2, 2, 4, 8), AXES)
    return jax.shard_map(
        on_device,
        mesh=torus,
        in_specs=(
            P(None, None, MP),
            P(),
            P(DP),
            P(None, MP),
            P(None, MP),
            P(AXES, None, None),
            P(AXES, None, None),
            P(AXES, None, None),
            P(AXES, None, None),
        ),
        out_specs=(P(AXES, None, None), P(None, DP, MP), P()),
        check_vma=False,
    )
```

time: 432 us -> 108 us (0.25); the launches traced: 424 us -> 106 us
  waiting for transfers between devices: 137 us -> 0 us
  local copies, waits for them, and re-layouts: 125 us -> 3.74 us
  blocking collectives: 105 us -> 0 us
  Pallas kernels: 0 us -> 102 us
  matrix products: 18.2 us -> 0 us
  starting transfers between devices: 16.1 us -> 0 us
  between operations: 14.6 us -> 0.65 us
  other arithmetic: 7.71 us -> 0 us
    pallas_call x0 -> x1, Pallas kernels: none -> 102 us  [on_device(): pl.pallas_call(kernel, out_shape=(jax.ShapeDtypeStruct((SEQ, D), BF16), j...]
    all_gather x1 -> x0, waiting for transfers between devices: 94.3 us -> none  [all_blocks(): blocks = lax.all_gather(blocks, axes[k], axis=0, tiled=True)]
    all_to_all x2 -> x0, blocking collectives: 43.7 us -> none  [the longest x1 33.9 us: on_device(): lax.all_to_all(outgoing_grads, MP, split_axis=3, concat_axis=0, tiled=True)]
    all_to_all x2 -> x0, waiting for transfers between devices: 43.1 us -> none  [the longest x1 22.6 us: sum_at_owner(): lax.all_to_all(blocks, axis, split_axis=0, concat_axis=0, tiled=True)]
    psum x5 -> x0, blocking collectives: 39.3 us -> none  [one_axis_at_a_time(): array = lax.psum(array, axis)]
    unnamed x44 -> x7, local copies, waits for them, and re-layouts: 40.8 us -> 3.74 us
    transpose x2 -> x0, local copies, waits for them, and re-layouts: 22.3 us -> none  [the longest x1 12 us: in_order(): blocks = jnp.moveaxis(blocks, 0, dim)]
    all_gather x2 -> x0, blocking collectives: 22 us -> none  [all_blocks(): blocks = lax.all_gather(blocks, axes[k], axis=0, tiled=True)]
  transfers between devices with their start and end apart: 3 -> 0, of which waited for: 3 -> 0; matrix products, arithmetic and copies ran while one was open for 4% -> 0% of each run, Pallas kernels for 0% -> 0%
where the time goes in v2:
time: 108 us; the launch traced here: 106 us
  Pallas kernels  102 us (94%)
  local copies, waits for them, and re-layouts  3.74 us (3%)
    pallas_call x1, Pallas kernels, on_device(): pl.pallas_call(kernel, out_shape=(jax.ShapeDtypeStruct((SEQ, D), BF16), j...  102 us
    unnamed x7, local copies, waits for them, and re-layouts  3.74 us

profile of v2, /device:TPU:8, one launch (start us, length us, event | category | flops | bytes accessed | tf_op | source)
XLA Modules:
  0.0 106.4 jit_solution(16880940617147965287)
XLA Ops:
  0.6 102.0 %prompt_step.1 = (bf16[128,4096]{1,0:T(8,128)(2,1)}, f32[16,64,128]{2,1,0:T(8,128)}, f32[8,128]{1,0:T(8,128)}) custom-call(s32[64]{0:T(128)} %tids.1, f32[8,128]{1,0:T(8,128)} %logits.1, bf16[64,64,128]{2,1,0:T(8,128)(2,1)} %bitcast.10, bf16[64,4096]{1,0:T(8,128)(2,1)} %bitcast.15, bf16[64,4096]{1,0:T(8,128)(2,1)} %bitcast.16, bf16[128,4096]{1,0:T(8,128)(2,1)} %bitcast.11, ...), custom_call_target="tpu_custom_call" | custom-call | tf_op jit(solution)/shard_map/prompt_step/pallas_call | solution.py:449
  102.7 0.0 copy-start
  102.7 2.3 %copy.15 = bf16[1,128,4096]{2,1,0:T(8,128)(2,1)} copy(bf16[1,128,4096]{2,1,0:T(8,128)(2,1)} %bitcast.9) | data formatting | bytes 2097152
  105.0 0.0 copy-done
  105.0 0.0 copy-start.1
  105.0 0.8 copy.16
  105.8 0.0 copy-done.1
  105.8 0.6 copy.17
Async XLA Ops:
  102.7 2.4 %copy-start = (f32[16,64,128]{2,1,0:T(8,128)S(1)}, f32[16,64,128]{2,1,0:T(8,128)}, u32[]{:S(2)}) copy-start(f32[16,64,128]{2,1,0:T(8,128)} %get-tuple-element.7) | copy-start | bytes 1572868
  105.0 0.8 copy-start.1

commit v3 on v2

v3 whole, which is shorter than its diff:
```python
import jax
import jax.numpy as jnp
from jax import lax
from jax.experimental import pallas as pl
from jax.experimental.pallas import tpu as pltpu
from jax.sharding import Mesh
from jax.sharding import PartitionSpec as P

D = 4096
HEADS = 32
DH = 128
NSRC = 128
NTASK = 8
PTOK = 64
SEQ = 128
AXES = ("dp_0", "dp_1", "mp_0", "mp_1", "mp_2")
MP = ("mp_0", "mp_1", "mp_2")
DP = ("dp_0", "dp_1")
MESH = pl.DeviceIdType.MESH
ROWS = 16
COLS = 64
PLANE = 32
F32 = jnp.float32
BF16 = jnp.bfloat16
HIGH = lax.Precision.HIGHEST


def here():
    return tuple(lax.axis_index(name) for name in AXES)


def push(src, dst, sent, landed, device):
    return pltpu.make_async_remote_copy(
        src_ref=src, dst_ref=dst, send_sem=sent, recv_sem=landed, device_id=device, device_id_type=MESH
    )


def drain(ref, sem):
    pltpu.make_async_copy(ref, ref, sem).wait()


def soft(logits):
    exponent = jnp.exp(logits - jnp.max(logits, axis=1, keepdims=True))
    return exponent / jnp.sum(exponent, axis=1, keepdims=True)


NN = (((1,), (0,)), ((), ()))
NT = (((1,), (1,)), ((), ()))
TN = (((0,), (0,)), ((), ()))
SCALE = DH ** (-0.5)
HOPS = (1, 2, 3, 0)
RING = (1, 7, 2, 6, 3, 5, 4)
PRE_HEADS = 2
MID_HEADS = 2
POST_HEADS = 2


def dot(a, b, dims=NN):
    return lax.dot_general(a, b, dims, preferred_element_type=F32)


def kernel(
    tids, logits, sp, kw, vw, queries, keys, values, cotangent,
    attended_hbm, source_grad_hbm, logits_grad,
    spv, w, qv, kv, vv, cv, mix_t, tb, tt, sel, out, pp, stat, self_e, pat, gg, rg, gz, rz, rt, ry, t2, rz2, sx, rx,
    wslot, wz, attended, source_grad,
    load_sem, store_sem, zs, zr, xs, xr, ys, yr, qs, qr, us, ur, ts, tr, ps, pr, gs, gr, bs, br, cs, cr, es, er, fs, fr,
    ws, wr, vs, vr,
):
    a, c, x, y, z = here()
    d, g = a * 2 + c, x * 4 + y
    me = d * 8 + g
    pair = lax.div(z, 2)
    barrier = pltpu.get_barrier_semaphore()

    def along(o, n, at):
        return lax.rem(at + o + n, n)

    d_ahead = [along(k, 4, d) for k in range(4)]
    d_behind = [along(-k, 4, d) for k in range(4)]
    g_behind = [along(-k, 8, g) for k in range(8)]
    partners = [(k, dd) for k in range(8) for dd in range(4)][1:]

    def device(d_to, g_to):
        return {
            "dp_0": lax.div(d_to, 2), "dp_1": lax.rem(d_to, 2), "mp_0": lax.div(g_to, 4), "mp_1": lax.rem(g_to, 4),
        }

    def at_z(to):
        return {"mp_2": to}

    def at_y(to):
        return {"mp_1": to}

    other = 1 - x
    x_peer = {"mp_0": other}

    def rows(quarter):
        return pl.ds(pl.multiple_of(quarter * ROWS, ROWS), ROWS)

    loads = [
        pltpu.make_async_copy(sp.at[pl.ds(d * ROWS, ROWS)], spv, load_sem.at[0]),
        pltpu.make_async_copy(queries, qv, load_sem.at[1]),
        pltpu.make_async_copy(keys, kv, load_sem.at[2]),
        pltpu.make_async_copy(cotangent, cv, load_sem.at[3]),
        pltpu.make_async_copy(values, vv, load_sem.at[4]),
        pltpu.make_async_copy(kw, w.at[pl.ds(0, COLS)], load_sem.at[5]),
        pltpu.make_async_copy(vw, w.at[pl.ds(COLS, COLS)], load_sem.at[6]),
    ]
    loads[0].start()
    for o in reversed(RING):
        pl.semaphore_signal(barrier, inc=1, device_id=at_z(along(o, 8, z)), device_id_type=MESH)
    for k, dd in partners:
        pl.semaphore_signal(barrier, inc=1, device_id=device(d_ahead[dd], g_behind[k]), device_id_type=MESH)
    for load in loads[1:]:
        load.start()
    tt[me] = jnp.full((8, 128), tids[x * 32 + y * 8 + z], jnp.int32).astype(F32)
    tile = jnp.concatenate([soft(logits[...]).astype(BF16).astype(F32)] * ROWS, axis=0)
    row = lax.broadcasted_iota(jnp.int32, (128, 128), 0)
    loads[0].wait()
    total = jnp.zeros((COLS, 128), F32)
    for r in range(ROWS):
        weights = jnp.where(row // NTASK == r, tile, 0.0).astype(BF16)
        total += dot(spv[r], weights, NT)
    mix_t[x, y, z] = total.astype(BF16)
    pl.semaphore_wait(barrier, PLANE - 1 + 7)

    own = mix_t.at[x, y, z]
    push(own, own, xs, xr, x_peer).start()
    for o in RING:
        push(own, own, zs, zr.at[0, o], at_z(along(o, 8, z))).start()
    for k, dd in partners:
        push(tt.at[me], tt.at[me], ts, tr, device(d_ahead[dd], g_behind[k])).start()
    own = mix_t.at[other, y, z]
    push(own, own, xs, xr, x_peer).wait_recv()
    for o in RING:
        push(own, own, zs, zr.at[1, o], at_z(along(o, 8, z))).start()

    def pre(first, count):
        masked = lax.broadcasted_iota(jnp.int32, (SEQ, SEQ), 0) > lax.broadcasted_iota(jnp.int32, (SEQ, SEQ), 1)

        def step(n, carry):
            for e in range(PRE_HEADS):
                h = first + n * PRE_HEADS + e
                lanes = pl.ds(pl.multiple_of(h * DH, DH), DH)
                scores = dot(kv[:, lanes], qv[:, lanes], NT) * SCALE
                scores = jnp.where(masked, -1e30, scores)
                top = jnp.max(scores, axis=0, keepdims=True)
                exponent = jnp.exp(scores - top)
                grad = dot(vv[:, lanes], cv[:, lanes], NT)
                self_e[h] = exponent
                stat[h, 0:1] = top
                stat[h, 1:2] = jnp.sum(exponent, axis=0, keepdims=True)
                stat[h, 2:3] = jnp.sum(exponent * grad, axis=0, keepdims=True)
            return carry

        lax.fori_loop(0, count // PRE_HEADS, step, 0)

    for load in loads[1:5]:
        load.wait()
    up, down, across = along(1, 4, y), along(-1, 4, y), along(2, 4, y)
    halves = (x, other)

    def project(half, at):
        columns = pl.ds(pl.multiple_of(half * 2048 + at * 512, 512), 512)
        return dot(w[:, columns], mix_t[half, at].reshape(512, 128))

    def y_push(n, half, o):
        block = mix_t.at[half, y, along(-o, 8, z)]
        push(block, block, ys, yr.at[n, 0, o], at_y(up)).start()
        push(block, block, ys, yr.at[n, 1, o], at_y(down)).start()

    def y_relay(n, half, o, upward):
        source = along(-o, 8, z)
        from_down, from_up = mix_t.at[half, down, source], mix_t.at[half, up, source]
        push(from_down, from_down, ys, yr.at[n, 0, o], at_y(down)).wait_recv()
        if upward:
            push(from_down, from_down, qs, qr.at[n], at_y(up)).start()
        push(from_up, from_up, ys, yr.at[n, 1, o], at_y(up)).wait_recv()
        if not upward:
            push(from_up, from_up, qs, qr.at[n], at_y(down)).start()

    y_push(0, x, 0)
    y_push(1, other, 0)
    pre(0, 6)
    for n, half in enumerate(halves):
        for o in RING:
            block = mix_t.at[half, y, along(-o, 8, z)]
            push(block, block, zs, zr.at[n, o], at_z(along(-o, 8, z))).wait_recv()
            y_push(n, half, o)
        if n == 0:
            for place, o in enumerate((0, *RING[:4])):
                y_relay(0, x, o, place % 2 == 0)
            pre(6, 4)
    for load in loads[5:]:
        load.wait()
    for place, o in enumerate(RING[4:]):
        y_relay(0, x, o, (place + 5) % 2 == 0)
    total = project(x, y) + project(x, down) + project(x, up) + project(other, y)

    drain(tt.at[pl.ds(0, PLANE - 1)], tr)
    lane = lax.broadcasted_iota(jnp.int32, (ROWS, 128), 1)
    prompt_row = lax.broadcasted_iota(jnp.int32, (ROWS, 128), 0)
    lane_task = (lane % NTASK).astype(F32)
    lane_row = lane // NTASK == prompt_row

    def select(p, carry):
        task = jnp.concatenate([tt[p], tt[p]], axis=0)
        hit = jnp.where(lane_row & (task == lane_task), 1.0, 0.0)
        sel[rows(p), :] = hit.astype(BF16)
        return carry

    for place, o in enumerate((0, *RING)):
        y_relay(1, other, o, place % 2 == 0)
    lax.fori_loop(0, PLANE, select, 0)
    total += project(other, down) + project(other, up)
    for n, half in enumerate(halves):
        drain(mix_t.at[half, across], qr.at[n])
        total += project(half, across)

    tb[z] = total.astype(BF16)
    mate = pair * 2 + 1 - lax.rem(z, 2)

    def u_send(to):
        push(tb.at[z], tb.at[z], us, ur.at[along(to - z, 8, 0)], at_z(to)).start()

    def u_wait(source):
        push(tb.at[source], tb.at[source], us, ur.at[along(z - source, 8, 0)], at_z(source)).wait_recv()

    for hop in HOPS:
        to = along(-hop, 4, pair)
        for one in (mate,) if hop == 0 else (2 * to, 2 * to + 1):
            u_send(one)

    own_rows = rows(d)
    pieces = [along(hop, 4, pair) for hop in HOPS]
    for j, i in enumerate(pieces):
        if j == 0:
            pre(10, 12)
        for one in (mate,) if HOPS[j] == 0 else (2 * i, 2 * i + 1):
            u_wait(one)
        for which in range(2):
            part = slice(which * COLS, (which + 1) * COLS)
            table = jnp.concatenate([tb[2 * i, part, :], tb[2 * i + 1, part, :]], axis=0)
            out[i, :, which] = dot(sel[...], table, NT).astype(BF16).reshape(PLANE, ROWS, DH)
        for k, dd in partners:
            d_to, g_to = d_ahead[dd], g_behind[k]
            push(
                out.at[i, d_to * 8 + g_to], pp.at[i, g, :, own_rows, :], ps, pr.at[j, k], device(d_to, g_to)
            ).start()
        for which in range(2):
            pp[i, g, which, own_rows, :] = out[i, me, which]
    pre(22, 10)

    def head(i, g_here):
        h = g_here * 4 + i
        lanes = pl.ds(pl.multiple_of(h * DH, DH), DH)
        q, cot = qv[:, lanes], cv[:, lanes]
        scores = dot(pp[i, g_here, 0], q, NT) * SCALE
        grad = dot(pp[i, g_here, 1], cot, NT)
        self_top = stat[h, 0:1]
        top = jnp.maximum(jnp.max(scores, axis=0, keepdims=True), self_top)
        exponent = jnp.exp(scores - top)
        shrink = jnp.exp(self_top - top)
        inverse = 1.0 / (shrink * stat[h, 1:2] + jnp.sum(exponent, axis=0, keepdims=True))
        attention = exponent * inverse
        self_scale = shrink * inverse
        stat[h, 3:4] = self_scale
        rounded = attention.astype(BF16)
        pat[h] = rounded
        inner = self_scale * stat[h, 2:3] + jnp.sum(attention * grad, axis=0, keepdims=True)
        grad_scores = (attention * (grad - inner)).astype(BF16)
        gg[i, g_here, 0] = (dot(grad_scores, q) * SCALE).astype(BF16)
        gg[i, g_here, 1] = dot(rounded, cot).astype(BF16)

    def mid_step(j, i, ks, own_first):
        groups = [along(k, 8, g) for k in ks]
        for n, (k, g_here) in enumerate(zip(ks, groups)):
            if own_first and n == 0:
                drain(pp.at[i, g_here, :, pl.ds(0, PTOK - ROWS), :], pr.at[j, k])
            else:
                drain(pp.at[i, g_here], pr.at[j, k])
        for g_here in groups:
            head(i, g_here)
        for n, g_here in enumerate(groups):
            for dd in range(1 if own_first and n == 0 else 0, 4):
                d_to = d_ahead[dd]
                push(
                    gg.at[i, g_here, :, rows(d_to), :], rg.at[i, me], gs, gr.at[j], device(d_to, g_here)
                ).start()

    for j, i in enumerate(pieces):
        mid_step(j, i, list(range(MID_HEADS)), True)
        rg[i, me] = gg[i, g, :, own_rows, :]

        def later(n, carry, j=j, i=i):
            mid_step(j, i, [n * MID_HEADS + e for e in range(MID_HEADS)], False)
            return carry

        lax.fori_loop(1, 8 // MID_HEADS, later, 0)

    def post(first, count):
        def step(n, carry):
            for e in range(POST_HEADS):
                h = first + n * POST_HEADS + e
                lanes = pl.ds(pl.multiple_of(h * DH, DH), DH)
                self_part = (self_e[h] * stat[h, 3:4]).astype(BF16)
                prompt_values = pp[lax.rem(h, 4), lax.div(h, 4), 1]
                summed = dot(self_part, vv[:, lanes], TN) + dot(pat[h], prompt_values, TN)
                attended[:, lanes] = summed.astype(BF16)
            return carry

        lax.fori_loop(0, count // POST_HEADS, step, 0)
        lanes = pl.ds(first * DH, count * DH)
        store = pltpu.make_async_copy(attended.at[:, lanes], attended_hbm.at[:, lanes], store_sem.at[len(stores)])
        store.start()
        stores.append(store)

    stores = []

    post(0, 8)

    for j, i in enumerate(pieces):
        drain(rg.at[i, pl.ds(0, PLANE - 1)], gr.at[j])
        for which in range(2):
            summed = dot(rg[i, :, which].reshape(PLANE * ROWS, DH), sel[...], TN).astype(BF16)
            part = slice(which * COLS, (which + 1) * COLS)
            gz[2 * i, part, :] = summed[:COLS]
            gz[2 * i + 1, part, :] = summed[COLS:]
        for to in (mate,) if HOPS[j] == 0 else (2 * i, 2 * i + 1):
            push(gz.at[to], rz.at[along(to - z, 8, 0)], bs, br, at_z(to)).start()
    post(8, 8)
    grad = gz[z].astype(F32)
    drain(rz.at[pl.ds(1, 7)], br)
    for o in range(1, 8):
        grad += rz[o].astype(F32)
    grad_high = grad.astype(BF16)
    grad_low = (grad - grad_high.astype(F32)).astype(BF16)
    grad_both = jnp.concatenate([grad_high, grad_low], axis=1)

    def row_terms(half, at):
        columns = pl.ds(pl.multiple_of(half * 2048 + at * 512, 512), 512)
        terms = dot(w[:, columns], grad_both, TN)
        rt[half, at] = (terms[:, :128] + terms[:, 128:]).astype(BF16).reshape(8, COLS, 128)

    halves = (other, x)
    for n, half in enumerate(halves):
        for o in (2, 1, 3):
            to = along(o, 4, y)
            row_terms(half, to)
            push(rt.at[half, to], ry.at[n, o], cs, cr.at[n, o], at_y(to)).start()
        row_terms(half, y)

    def y_sum(n, half):
        four = rt[half, y].astype(F32)
        for o in (1, 3, 2):
            push(rt.at[half, y], ry.at[n, o], cs, cr.at[n, o], at_y(along(-o, 4, y))).wait_recv()
            four += ry[n, o].astype(F32)
        t2[n] = four.astype(BF16)
        for o in reversed(RING):
            to = along(o, 8, z)
            push(t2.at[n, to], rz2.at[n, o], es, er.at[n], at_z(to)).start()

    def z_sum(n):
        eight = t2[n, z].astype(F32)
        drain(rz2.at[n, pl.ds(1, 7)], er.at[n])
        for o in range(1, 8):
            eight += rz2[n, o].astype(F32)
        return eight

    post(16, 12)
    y_sum(0, other)
    y_sum(1, x)
    sx[...] = z_sum(0)
    push(sx, rx, fs, fr, x_peer).start()
    post(28, 4)
    mix = soft(logits[...])
    mine = z_sum(1)
    drain(rx, fr)
    mixture_grad = mine + rx[...]

    flipped = mixture_grad.T
    part = jnp.zeros((NTASK, NSRC), F32)
    for r in range(ROWS):
        part += jnp.dot(
            flipped[r * NTASK : (r + 1) * NTASK], spv[r].astype(F32), precision=HIGH, preferred_element_type=F32
        )
    wslot[me] = part

    for k, dd in partners:
        push(wslot.at[me], wslot.at[me], ws, wr, device(d_ahead[dd], g_behind[k])).start()
    tile = jnp.concatenate([mix] * ROWS, axis=0)
    lane = lax.broadcasted_iota(jnp.int32, (COLS, 128), 1)
    for r in range(ROWS):
        chosen = jnp.where(lane // NTASK == r, mixture_grad, 0.0)
        source_grad[r] = jnp.dot(chosen, tile, precision=HIGH, preferred_element_type=F32)
    store = pltpu.make_async_copy(source_grad, source_grad_hbm, store_sem.at[len(stores)])
    store.start()
    stores.append(store)
    drain(wslot.at[pl.ds(0, PLANE - 1)], wr)
    wz[z] = jnp.sum(wslot[...], axis=0)
    for o in reversed(RING):
        push(wz.at[z], wz.at[z], vs, vr, at_z(along(o, 8, z))).start()
    drain(mix_t.at[0, y, z], xs)
    drain(mix_t.at[:, y, pl.ds(0, 7)], zs)
    drain(mix_t.at[:, pl.ds(0, 2)], ys)
    drain(mix_t.at[:, y], qs)
    drain(tt.at[pl.ds(0, PLANE - 1)], ts)
    drain(tb.at[pl.ds(0, 7)], us)
    drain(out.at[:, pl.ds(0, PLANE - 1)], ps)
    drain(rg.at[:, pl.ds(0, PLANE - 1)], gs)
    drain(gz.at[pl.ds(0, 7)], bs)
    drain(rt.at[:, pl.ds(0, 3)], cs)
    drain(t2.at[:, pl.ds(0, 7)], es)
    drain(sx, fs)
    drain(wslot.at[pl.ds(0, PLANE - 1)], ws)
    for store in stores:
        store.wait()
    drain(wz.at[pl.ds(0, 7)], vr)
    weight_grad = jnp.sum(wz[...], axis=0)
    logits_grad[...] = mix * (weight_grad - jnp.sum(mix * weight_grad, axis=1, keepdims=True))
    drain(wz.at[pl.ds(0, 7)], vs)


PARTS = 4


def finish_kernel(attended_in, source_in, logits_in, attended_out, source_out, logits_out, held, tile, came, left):
    def parts(src, dst, sems):
        ends = ((src[0], dst[0], SEQ // PARTS), (src[1], dst[1], ROWS // PARTS))
        return [
            pltpu.make_async_copy(one.at[pl.ds(n * size, size)], to.at[pl.ds(n * size, size)], sems.at[k * PARTS + n])
            for k, (one, to, size) in enumerate(ends)
            for n in range(PARTS)
        ]

    arriving = parts((attended_in, source_in), (held, tile), came)
    leaving = parts((held, tile), (attended_out, source_out), left)
    for one in arriving:
        one.start()
    logits_out[...] = logits_in[...]
    for one, two in zip(arriving, leaving):
        one.wait()
        two.start()
    for two in leaving:
        two.wait()


def finish(attended, source_grad, logits_grad):
    any_space = pl.BlockSpec(memory_space=pl.ANY)
    vmem = pl.BlockSpec(memory_space=pltpu.VMEM)
    given = (attended, source_grad, logits_grad)
    return pl.pallas_call(
        finish_kernel,
        out_shape=tuple(jax.ShapeDtypeStruct(one.shape, one.dtype) for one in given),
        in_specs=[any_space, any_space, vmem],
        out_specs=(any_space, any_space, vmem),
        scratch_shapes=[
            pltpu.VMEM(attended.shape, BF16),
            pltpu.VMEM(source_grad.shape, F32),
            pltpu.SemaphoreType.DMA((2 * PARTS,)),
            pltpu.SemaphoreType.DMA((2 * PARTS,)),
        ],
        name="prompt_finish",
    )(*given)


def on_device(source_prompts, task_logits, task_ids, key_weight, value_weight, queries, keys, values, cotangent):
    any_space = pl.BlockSpec(memory_space=pl.ANY)
    vmem = pl.BlockSpec(memory_space=pltpu.VMEM)
    dma = pltpu.SemaphoreType.DMA
    block = (2, 8, COLS, 128)
    attended, source_grad, logits_grad = pl.pallas_call(
        kernel,
        out_shape=(
            jax.ShapeDtypeStruct((SEQ, D), BF16),
            jax.ShapeDtypeStruct((ROWS, COLS, NSRC), F32),
            jax.ShapeDtypeStruct((NTASK, NSRC), F32),
        ),
        in_specs=[pl.BlockSpec(memory_space=pltpu.SMEM), vmem] + [any_space] * 7,
        out_specs=(any_space, any_space, vmem),
        scratch_shapes=[
            pltpu.VMEM((ROWS, COLS, NSRC), BF16),
            pltpu.VMEM((2 * COLS, D), BF16),
            *[pltpu.VMEM((SEQ, D), BF16)] * 4,
            pltpu.VMEM((2, 4, 8, COLS, 128), BF16),
            pltpu.VMEM((8, 128, 128), BF16),
            pltpu.VMEM((PLANE, 8, 128), F32),
            pltpu.VMEM((PLANE * ROWS, 128), BF16),
            pltpu.VMEM((4, PLANE, 2, ROWS, DH), BF16),
            pltpu.VMEM((4, 8, 2, PTOK, DH), BF16),
            pltpu.VMEM((HEADS, 8, SEQ), F32),
            pltpu.VMEM((HEADS, SEQ, SEQ), F32),
            pltpu.VMEM((HEADS, PTOK, SEQ), BF16),
            pltpu.VMEM((4, 8, 2, PTOK, DH), BF16),
            pltpu.VMEM((4, PLANE, 2, ROWS, DH), BF16),
            pltpu.VMEM((8, 128, 128), BF16),
            pltpu.VMEM((8, 128, 128), BF16),
            pltpu.VMEM((2, 4, 8, COLS, 128), BF16),
            pltpu.VMEM((2, 4, 8, COLS, 128), BF16),
            pltpu.VMEM(block, BF16),
            pltpu.VMEM(block, BF16),
            pltpu.VMEM((COLS, 128), F32),
            pltpu.VMEM((COLS, 128), F32),
            pltpu.VMEM((PLANE, NTASK, NSRC), F32),
            pltpu.VMEM((8, NTASK, NSRC), F32),
            pltpu.VMEM((SEQ, D), BF16),
            pltpu.VMEM((ROWS, COLS, NSRC), F32),
            dma((7,)), dma((5,)), dma, dma((2, 8)), dma, dma, dma, dma((2, 2, 8)), dma, dma((2,)), dma, dma((8,)),
            dma, dma, dma, dma((4, 8)), dma, dma((4,)), dma, dma, dma, dma((2, 4)), dma, dma((2,)), dma, dma,
            dma, dma, dma, dma,
        ],
        compiler_params=pltpu.CompilerParams(collective_id=0, has_side_effects=True),
        name="prompt_step",
    )(
        task_ids, task_logits, source_prompts.transpose(1, 2, 0), key_weight.T, value_weight.T,
        queries[0], keys[0], values[0], cotangent[0],
    )
    attended, source_grad, logits_grad = finish(attended, source_grad, logits_grad)
    return attended[None], source_grad.transpose(2, 0, 1), logits_grad


def solution(mesh):
    torus = Mesh(mesh.devices.reshape(2, 2, 2, 4, 8), AXES)
    return jax.shard_map(
        on_device,
        mesh=torus,
        in_specs=(
            P(None, None, MP),
            P(),
            P(DP),
            P(None, MP),
            P(None, MP),
            P(AXES, None, None),
            P(AXES, None, None),
            P(AXES, None, None),
            P(AXES, None, None),
        ),
        out_specs=(P(AXES, None, None), P(None, DP, MP), P()),
        check_vma=False,
    )
```

time: 108 us -> 97.2 us (0.900)
  Pallas kernels: 102 us -> 95.3 us
  local copies, waits for them, and re-layouts: 3.74 us -> 0 us
    pallas_call x1, Pallas kernels: 102 us -> 91.8 us  [on_device(): pl.pallas_call(kernel, out_shape=(jax.ShapeDtypeStruct((SEQ, D), BF16), j...]
    unnamed x7 -> x0, local copies, waits for them, and re-layouts: 3.74 us -> none
    pallas_call x0 -> x1, Pallas kernels: none -> 3.48 us  [finish(): pl.pallas_call(finish_kernel, out_shape=tuple((jax.ShapeDtypeStruct(one.s...]
where the time goes in v3:
time: 97.2 us; the launch traced here: 95.9 us
  Pallas kernels  95.3 us (98%)
    pallas_call x1, Pallas kernels, on_device(): pl.pallas_call(kernel, out_shape=(jax.ShapeDtypeStruct((SEQ, D), BF16), j...  91.8 us
    pallas_call x1, Pallas kernels, finish(): pl.pallas_call(finish_kernel, out_shape=tuple((jax.ShapeDtypeStruct(one.s...  3.48 us

profile of v3, /device:TPU:8, one launch (start us, length us, event | category | flops | bytes accessed | tf_op | source)
XLA Modules:
  0.0 95.9 jit_solution(680847292162051526)
XLA Ops:
  0.6 91.8 %prompt_step.1 = (bf16[128,4096]{1,0:T(8,128)(2,1)}, f32[16,64,128]{2,1,0:T(8,128)}, f32[8,128]{1,0:T(8,128)}) custom-call(s32[64]{0:T(128)} %tids.1, f32[8,128]{1,0:T(8,128)} %logits.1, bf16[64,64,128]{2,1,0:T(8,128)(2,1)} %bitcast.9, bf16[64,4096]{1,0:T(8,128)(2,1)} %bitcast.14, bf16[64,4096]{1,0:T(8,128)(2,1)} %bitcast.15, bf16[128,4096]{1,0:T(8,128)(2,1)} %bitcast.10, ...), custom_call_target="tpu_custom_call" | custom-call | tf_op jit(solution)/shard_map/prompt_step/pallas_call | solution.py:473
  92.4 3.5 %prompt_finish.1 = (bf16[128,4096]{1,0:T(8,128)(2,1)}, f32[16,64,128]{2,1,0:T(8,128)}, f32[8,128]{1,0:T(8,128)}) custom-call(bf16[128,4096]{1,0:T(8,128)(2,1)} %get-tuple-element.9.attended_in, f32[16,64,128]{2,1,0:T(8,128)} %get-tuple-element.10.source_in, f32[8,128]{1,0:T(8,128)} %get-tuple-element.11.logits_in), custom_call_target="tpu_custom_call" | custom-call | tf_op jit(solution)/shard_map/prompt_finish/pallas_call | solution.py:453

commit v4 on v3

--- a/solution.py
+++ b/solution.py
@@ -39,6 +39,11 @@
     pltpu.make_async_copy(ref, ref, sem).wait()
 
 
+def far(partner):
+    k, dd = partner
+    return min(k % 4, 4 - k % 4) + (dd // 2) * 2 + k // 4
+
+
 def soft(logits):
     exponent = jnp.exp(logits - jnp.max(logits, axis=1, keepdims=True))
     return exponent / jnp.sum(exponent, axis=1, keepdims=True)
@@ -48,7 +53,8 @@
 NT = (((1,), (1,)), ((), ()))
 TN = (((0,), (0,)), ((), ()))
 SCALE = DH ** (-0.5)
-HOPS = (1, 2, 3, 0)
+HOPS = (0, 1, 3, 2)
+MID = (1, 2, 3, 0)
 RING = (1, 7, 2, 6, 3, 5, 4)
 PRE_HEADS = 2
 MID_HEADS = 2
@@ -61,10 +67,10 @@
 
 def kernel(
     tids, logits, sp, kw, vw, queries, keys, values, cotangent,
-    attended_hbm, source_grad_hbm, logits_grad,
-    spv, w, qv, kv, vv, cv, mix_t, tb, tt, sel, out, pp, stat, self_e, pat, gg, rg, gz, rz, rt, ry, t2, rz2, sx, rx,
-    wslot, wz, attended, source_grad,
-    load_sem, store_sem, zs, zr, xs, xr, ys, yr, qs, qr, us, ur, ts, tr, ps, pr, gs, gr, bs, br, cs, cr, es, er, fs, fr,
+    attended, source_grad, logits_grad,
+    spv, w, qv, kv, vv, cv, mix_t, tb, tt, sel, out, pp, stat, self_e, pat, gg, rg, gz, rz, rt, rl, ry, t2, rz2, sx, rx,
+    wslot, wz,
+    load_sem, zs, zr, xs, xr, ys, yr, qs, qr, us, ur, ts, tr, ps, pr, gs, gr, bs, br, cs, lr, cr, es, er, fs, fr,
     ws, wr, vs, vr,
 ):
     a, c, x, y, z = here()
@@ -110,7 +116,7 @@
     loads[0].start()
     for o in reversed(RING):
         pl.semaphore_signal(barrier, inc=1, device_id=at_z(along(o, 8, z)), device_id_type=MESH)
-    for k, dd in partners:
+    for k, dd in sorted(partners, key=far, reverse=True):
         pl.semaphore_signal(barrier, inc=1, device_id=device(d_ahead[dd], g_behind[k]), device_id_type=MESH)
     for load in loads[1:]:
         load.start()
@@ -183,20 +189,22 @@
     y_push(0, x, 0)
     y_push(1, other, 0)
     pre(0, 6)
-    for n, half in enumerate(halves):
-        for o in RING:
+    for o in RING:
+        for n, half in enumerate(halves):
             block = mix_t.at[half, y, along(-o, 8, z)]
             push(block, block, zs, zr.at[n, o], at_z(along(-o, 8, z))).wait_recv()
             y_push(n, half, o)
-        if n == 0:
-            for place, o in enumerate((0, *RING[:4])):
-                y_relay(0, x, o, place % 2 == 0)
-            pre(6, 4)
+    places = tuple(enumerate((0, *RING)))
+    for place, o in places[:6]:
+        for n, half in enumerate(halves):
+            y_relay(n, half, o, place % 2 == 0)
     for load in loads[5:]:
         load.wait()
-    for place, o in enumerate(RING[4:]):
-        y_relay(0, x, o, (place + 5) % 2 == 0)
-    total = project(x, y) + project(x, down) + project(x, up) + project(other, y)
+    total = project(x, y) + project(other, y)
+    for place, o in places[6:]:
+        for n, half in enumerate(halves):
+            y_relay(n, half, o, place % 2 == 0)
+    total += project(x, down) + project(x, up) + project(other, down) + project(other, up)
 
     drain(tt.at[pl.ds(0, PLANE - 1)], tr)
     lane = lax.broadcasted_iota(jnp.int32, (ROWS, 128), 1)
@@ -210,10 +218,7 @@
         sel[rows(p), :] = hit.astype(BF16)
         return carry
 
-    for place, o in enumerate((0, *RING)):
-        y_relay(1, other, o, place % 2 == 0)
     lax.fori_loop(0, PLANE, select, 0)
-    total += project(other, down) + project(other, up)
     for n, half in enumerate(halves):
         drain(mix_t.at[half, across], qr.at[n])
         total += project(half, across)
@@ -236,7 +241,7 @@
     pieces = [along(hop, 4, pair) for hop in HOPS]
     for j, i in enumerate(pieces):
         if j == 0:
-            pre(10, 12)
+            pre(6, 12)
         for one in (mate,) if HOPS[j] == 0 else (2 * i, 2 * i + 1):
             u_wait(one)
         for which in range(2):
@@ -250,7 +255,7 @@
             ).start()
         for which in range(2):
             pp[i, g, which, own_rows, :] = out[i, me, which]
-    pre(22, 10)
+    pre(18, 14)
 
     def head(i, g_here):
         h = g_here * 4 + i
@@ -289,7 +294,8 @@
                     gg.at[i, g_here, :, rows(d_to), :], rg.at[i, me], gs, gr.at[j], device(d_to, g_here)
                 ).start()
 
-    for j, i in enumerate(pieces):
+    for j in MID:
+        i = pieces[j]
         mid_step(j, i, list(range(MID_HEADS)), True)
         rg[i, me] = gg[i, g, :, own_rows, :]
 
@@ -311,16 +317,11 @@
             return carry
 
         lax.fori_loop(0, count // POST_HEADS, step, 0)
-        lanes = pl.ds(first * DH, count * DH)
-        store = pltpu.make_async_copy(attended.at[:, lanes], attended_hbm.at[:, lanes], store_sem.at[len(stores)])
-        store.start()
-        stores.append(store)
-
-    stores = []
 
     post(0, 8)
 
-    for j, i in enumerate(pieces):
+    for j in MID:
+        i = pieces[j]
         drain(rg.at[i, pl.ds(0, PLANE - 1)], gr.at[j])
         for which in range(2):
             summed = dot(rg[i, :, which].reshape(PLANE * ROWS, DH), sel[...], TN).astype(BF16)
@@ -341,41 +342,67 @@
     def row_terms(half, at):
         columns = pl.ds(pl.multiple_of(half * 2048 + at * 512, 512), 512)
         terms = dot(w[:, columns], grad_both, TN)
-        rt[half, at] = (terms[:, :128] + terms[:, 128:]).astype(BF16).reshape(8, COLS, 128)
-
-    halves = (other, x)
-    for n, half in enumerate(halves):
-        for o in (2, 1, 3):
-            to = along(o, 4, y)
-            row_terms(half, to)
-            push(rt.at[half, to], ry.at[n, o], cs, cr.at[n, o], at_y(to)).start()
+        terms = (terms[:, :128] + terms[:, 128:]).astype(BF16).reshape(8, 2, COLS // 2, 128)
+        for part in range(2):
+            rt[half, part, at] = terms[:, part]
+
+    def y_send(src, dst, landed, to):
+        push(src, dst, cs, landed, at_y(to)).start()
+
+    first, last = pl.ds(0, 4), pl.ds(4, 4)
+    chunks = [(n, half, part) for n, half in enumerate((other, x)) for part in range(2)]
+    for n, half in enumerate((other, x)):
+        row_terms(half, across)
+        for part in range(2):
+            y_send(rt.at[half, part, across, first], rl.at[n, part, 0], lr.at[n, part, 0], up)
+            y_send(rt.at[half, part, across, last], rl.at[n, part, 1], lr.at[n, part, 1], down)
+        row_terms(half, up)
+        for part in range(2):
+            y_send(rt.at[half, part, up, last], ry.at[n, part, 0, last], cr.at[n, part, 0], up)
+        row_terms(half, down)
+        for part in range(2):
+            y_send(rt.at[half, part, down, first], ry.at[n, part, 1, first], cr.at[n, part, 1], down)
+    for half in (other, x):
         row_terms(half, y)
 
-    def y_sum(n, half):
-        four = rt[half, y].astype(F32)
-        for o in (1, 3, 2):
-            push(rt.at[half, y], ry.at[n, o], cs, cr.at[n, o], at_y(along(-o, 4, y))).wait_recv()
-            four += ry[n, o].astype(F32)
-        t2[n] = four.astype(BF16)
+    def y_add(n, half, part):
+        for way, to, piece in ((0, up, slice(0, 4)), (1, down, slice(4, 8))):
+            drain(rl.at[n, part, way], lr.at[n, part, way])
+            joined = rt[half, part, to, piece].astype(F32) + rl[n, part, way].astype(F32)
+            rt[half, part, to, piece] = joined.astype(BF16)
+            section = first if way == 0 else last
+            y_send(rt.at[half, part, to, section], ry.at[n, part, way, section], cr.at[n, part, way], to)
+
+    def y_sum(n, half, part):
+        three = rt[half, part, y].astype(F32)
+        for way in range(2):
+            drain(ry.at[n, part, way], cr.at[n, part, way])
+            three += ry[n, part, way].astype(F32)
+        t2[n, part] = three.astype(BF16)
         for o in reversed(RING):
             to = along(o, 8, z)
-            push(t2.at[n, to], rz2.at[n, o], es, er.at[n], at_z(to)).start()
-
-    def z_sum(n):
-        eight = t2[n, z].astype(F32)
-        drain(rz2.at[n, pl.ds(1, 7)], er.at[n])
+            push(t2.at[n, part, to], rz2.at[n, part, o], es, er.at[n, part], at_z(to)).start()
+
+    def z_sum(n, part):
+        eight = t2[n, part, z].astype(F32)
+        drain(rz2.at[n, part, pl.ds(1, 7)], er.at[n, part])
         for o in range(1, 8):
-            eight += rz2[n, o].astype(F32)
+            eight += rz2[n, part, o].astype(F32)
         return eight
 
-    post(16, 12)
-    y_sum(0, other)
-    y_sum(1, x)
-    sx[...] = z_sum(0)
+    y_add(*chunks[0])
+    y_add(*chunks[1])
+    post(16, 6)
+    y_add(*chunks[2])
+    y_add(*chunks[3])
+    post(22, 10)
+    for chunk in chunks:
+        y_sum(*chunk)
+    mix = soft(logits[...])
+    for part in range(2):
+        sx[part * 32 : (part + 1) * 32] = z_sum(0, part)
     push(sx, rx, fs, fr, x_peer).start()
-    post(28, 4)
-    mix = soft(logits[...])
-    mine = z_sum(1)
+    mine = jnp.concatenate([z_sum(1, 0), z_sum(1, 1)], axis=0)
     drain(rx, fr)
     mixture_grad = mine + rx[...]
 
@@ -394,9 +421,6 @@
     for r in range(ROWS):
         chosen = jnp.where(lane // NTASK == r, mixture_grad, 0.0)
         source_grad[r] = jnp.dot(chosen, tile, precision=HIGH, preferred_element_type=F32)
-    store = pltpu.make_async_copy(source_grad, source_grad_hbm, store_sem.at[len(stores)])
-    store.start()
-    stores.append(store)
     drain(wslot.at[pl.ds(0, PLANE - 1)], wr)
     wz[z] = jnp.sum(wslot[...], axis=0)
     for o in reversed(RING):
@@ -410,75 +434,30 @@
     drain(out.at[:, pl.ds(0, PLANE - 1)], ps)
     drain(rg.at[:, pl.ds(0, PLANE - 1)], gs)
     drain(gz.at[pl.ds(0, 7)], bs)
-    drain(rt.at[:, pl.ds(0, 3)], cs)
-    drain(t2.at[:, pl.ds(0, 7)], es)
+    drain(rt.at[:, :, pl.ds(0, 3)], cs)
+    drain(t2.at[:, :, pl.ds(0, 7)], es)
     drain(sx, fs)
     drain(wslot.at[pl.ds(0, PLANE - 1)], ws)
-    for store in stores:
-        store.wait()
     drain(wz.at[pl.ds(0, 7)], vr)
     weight_grad = jnp.sum(wz[...], axis=0)
     logits_grad[...] = mix * (weight_grad - jnp.sum(mix * weight_grad, axis=1, keepdims=True))
     drain(wz.at[pl.ds(0, 7)], vs)
 
 
-PARTS = 4
-
-
-def finish_kernel(attended_in, source_in, logits_in, attended_out, source_out, logits_out, held, tile, came, left):
-    def parts(src, dst, sems):
-        ends = ((src[0], dst[0], SEQ // PARTS), (src[1], dst[1], ROWS // PARTS))
-        return [
-            pltpu.make_async_copy(one.at[pl.ds(n * size, size)], to.at[pl.ds(n * size, size)], sems.at[k * PARTS + n])
-            for k, (one, to, size) in enumerate(ends)
-            for n in range(PARTS)
-        ]
-
-    arriving = parts((attended_in, source_in), (held, tile), came)
-    leaving = parts((held, tile), (attended_out, source_out), left)
-    for one in arriving:
-        one.start()
-    logits_out[...] = logits_in[...]
-    for one, two in zip(arriving, leaving):
-        one.wait()
-        two.start()
-    for two in leaving:
-        two.wait()
-
-
-def finish(attended, source_grad, logits_grad):
-    any_space = pl.BlockSpec(memory_space=pl.ANY)
-    vmem = pl.BlockSpec(memory_space=pltpu.VMEM)
-    given = (attended, source_grad, logits_grad)
-    return pl.pallas_call(
-        finish_kernel,
-        out_shape=tuple(jax.ShapeDtypeStruct(one.shape, one.dtype) for one in given),
-        in_specs=[any_space, any_space, vmem],
-        out_specs=(any_space, any_space, vmem),
-        scratch_shapes=[
-            pltpu.VMEM(attended.shape, BF16),
-            pltpu.VMEM(source_grad.shape, F32),
-            pltpu.SemaphoreType.DMA((2 * PARTS,)),
-            pltpu.SemaphoreType.DMA((2 * PARTS,)),
-        ],
-        name="prompt_finish",
-    )(*given)
-
-
 def on_device(source_prompts, task_logits, task_ids, key_weight, value_weight, queries, keys, values, cotangent):
     any_space = pl.BlockSpec(memory_space=pl.ANY)
     vmem = pl.BlockSpec(memory_space=pltpu.VMEM)
     dma = pltpu.SemaphoreType.DMA
-    block = (2, 8, COLS, 128)
+    block = (8, COLS // 2, 128)
     attended, source_grad, logits_grad = pl.pallas_call(
         kernel,
         out_shape=(
-            jax.ShapeDtypeStruct((SEQ, D), BF16),
-            jax.ShapeDtypeStruct((ROWS, COLS, NSRC), F32),
-            jax.ShapeDtypeStruct((NTASK, NSRC), F32),
+            pltpu.VMEM((SEQ, D), BF16),
+            pltpu.VMEM((ROWS, COLS, NSRC), F32),
+            pltpu.VMEM((NTASK, NSRC), F32),
         ),
         in_specs=[pl.BlockSpec(memory_space=pltpu.SMEM), vmem] + [any_space] * 7,
-        out_specs=(any_space, any_space, vmem),
+        out_specs=(vmem, vmem, vmem),
         scratch_shapes=[
             pltpu.VMEM((ROWS, COLS, NSRC), BF16),
             pltpu.VMEM((2 * COLS, D), BF16),
@@ -496,18 +475,17 @@
             pltpu.VMEM((4, PLANE, 2, ROWS, DH), BF16),
             pltpu.VMEM((8, 128, 128), BF16),
             pltpu.VMEM((8, 128, 128), BF16),
-            pltpu.VMEM((2, 4, 8, COLS, 128), BF16),
-            pltpu.VMEM((2, 4, 8, COLS, 128), BF16),
-            pltpu.VMEM(block, BF16),
-            pltpu.VMEM(block, BF16),
+            pltpu.VMEM((2, 2, 4, *block), BF16),
+            pltpu.VMEM((2, 2, 2, 4, COLS // 2, 128), BF16),
+            pltpu.VMEM((2, 2, 2, *block), BF16),
+            pltpu.VMEM((2, 2, *block), BF16),
+            pltpu.VMEM((2, 2, *block), BF16),
             pltpu.VMEM((COLS, 128), F32),
             pltpu.VMEM((COLS, 128), F32),
             pltpu.VMEM((PLANE, NTASK, NSRC), F32),
             pltpu.VMEM((8, NTASK, NSRC), F32),
-            pltpu.VMEM((SEQ, D), BF16),
-            pltpu.VMEM((ROWS, COLS, NSRC), F32),
-            dma((7,)), dma((5,)), dma, dma((2, 8)), dma, dma, dma, dma((2, 2, 8)), dma, dma((2,)), dma, dma((8,)),
-            dma, dma, dma, dma((4, 8)), dma, dma((4,)), dma, dma, dma, dma((2, 4)), dma, dma((2,)), dma, dma,
+            dma((7,)), dma, dma((2, 8)), dma, dma, dma, dma((2, 2, 8)), dma, dma((2,)), dma, dma((8,)),
+            dma, dma, dma, dma((4, 8)), dma, dma((4,)), dma, dma, dma, dma((2, 2, 2)), dma((2, 2, 2)), dma, dma((2, 2)), dma, dma,
             dma, dma, dma, dma,
         ],
         compiler_params=pltpu.CompilerParams(collective_id=0, has_side_effects=True),
@@ -516,7 +494,6 @@
         task_ids, task_logits, source_prompts.transpose(1, 2, 0), key_weight.T, value_weight.T,
         queries[0], keys[0], values[0], cotangent[0],
     )
-    attended, source_grad, logits_grad = finish(attended, source_grad, logits_grad)
     return attended[None], source_grad.transpose(2, 0, 1), logits_grad
 
 

time: 97.2 us -> 94.4 us (0.971)
  Pallas kernels: 95.3 us -> 90.2 us
  local copies, waits for them, and re-layouts: 0 us -> 2.36 us
    pallas_call x2 -> x1, Pallas kernels: 95.3 us -> 90.2 us  [on_device(): pl.pallas_call(kernel, out_shape=(pltpu.VMEM((SEQ, D), BF16), pltpu.VMEM(...]
    unnamed x0 -> x3, local copies, waits for them, and re-layouts: none -> 2.36 us
where the time goes in v4:
time: 94.4 us; the launch traced here: 93.2 us
  Pallas kernels  90.2 us (96%)
  local copies, waits for them, and re-layouts  2.36 us (2%)
    pallas_call x1, Pallas kernels, on_device(): pl.pallas_call(kernel, out_shape=(pltpu.VMEM((SEQ, D), BF16), pltpu.VMEM(...  90.2 us
    unnamed x3, local copies, waits for them, and re-layouts  2.36 us

profile of v4, /device:TPU:8, one launch (start us, length us, event | category | flops | bytes accessed | tf_op | source)
XLA Modules:
  0.0 93.2 jit_solution(7224706208727665796)
XLA Ops:
  0.6 90.2 %prompt_step.1 = (bf16[128,4096]{1,0:T(8,128)(2,1)S(1)}, f32[16,64,128]{2,1,0:T(8,128)S(1)}, f32[8,128]{1,0:T(8,128)S(1)}) custom-call(s32[64]{0:T(128)} %tids.1, f32[8,128]{1,0:T(8,128)} %logits.1, bf16[64,64,128]{2,1,0:T(8,128)(2,1)} %bitcast.11, bf16[64,4096]{1,0:T(8,128)(2,1)} %bitcast.16, bf16[64,4096]{1,0:T(8,128)(2,1)} %bitcast.17, ...), custom_call_target="tpu_custom_call" | custom-call | tf_op jit(solution)/shard_map/prompt_step/pallas_call | solution.py:452
  90.9 1.0 %copy.15 = bf16[1,128,4096]{2,1,0:T(8,128)(2,1)} copy(bf16[1,128,4096]{2,1,0:T(8,128)(2,1)S(1)} %bitcast.9) | data formatting | bytes 2097152
  91.8 0.8 copy.16
  92.6 0.6 copy.17

commit v5 on v4

--- a/solution.py
+++ b/solution.py
@@ -56,6 +56,7 @@
 HOPS = (0, 1, 3, 2)
 MID = (1, 2, 3, 0)
 RING = (1, 7, 2, 6, 3, 5, 4)
+EARLY, LATE = (1, 7, 4, 3), (2, 6, 5)
 PRE_HEADS = 2
 MID_HEADS = 2
 POST_HEADS = 2
@@ -68,9 +69,9 @@
 def kernel(
     tids, logits, sp, kw, vw, queries, keys, values, cotangent,
     attended, source_grad, logits_grad,
-    spv, w, qv, kv, vv, cv, mix_t, tb, tt, sel, out, pp, stat, self_e, pat, gg, rg, gz, rz, rt, rl, ry, t2, rz2, sx, rx,
+    spv, w, wx, qv, kv, vv, cv, mix_t, tb, tt, sel, out, pp, stat, self_e, pat, gg, rg, gz, rz, gt, t2, rz2,
     wslot, wz,
-    load_sem, zs, zr, xs, xr, ys, yr, qs, qr, us, ur, ts, tr, ps, pr, gs, gr, bs, br, cs, lr, cr, es, er, fs, fr,
+    load_sem, zs, zr, xs, xr, ys, yr, qs, qr, us, ur, ts, tr, ps, pr, gs, gr, hs, hr, ks, kr, bs, br, cs, cr, es, er,
     ws, wr, vs, vr,
 ):
     a, c, x, y, z = here()
@@ -85,6 +86,7 @@
     d_ahead = [along(k, 4, d) for k in range(4)]
     d_behind = [along(-k, 4, d) for k in range(4)]
     g_behind = [along(-k, 8, g) for k in range(8)]
+    g_ahead = [along(k, 8, g) for k in range(8)]
     partners = [(k, dd) for k in range(8) for dd in range(4)][1:]
 
     def device(d_to, g_to):
@@ -94,6 +96,9 @@
 
     def at_z(to):
         return {"mp_2": to}
+
+    def at_g(to):
+        return {"mp_0": lax.div(to, 4), "mp_1": lax.rem(to, 4)}
 
     def at_y(to):
         return {"mp_1": to}
@@ -237,6 +242,24 @@
         for one in (mate,) if hop == 0 else (2 * to, 2 * to + 1):
             u_send(one)
 
+    half = pl.ds(pl.multiple_of(c * COLS, COLS), COLS)
+    missing = pl.ds(pl.multiple_of((1 - c) * COLS, COLS), COLS)
+
+    def features(at):
+        return pl.ds(pl.multiple_of(at * 512, 512), 512)
+
+    def fetch(k):
+        to = g_behind[k]
+        push(w.at[half, features(to)], wx.at[g, half], hs, hr.at[k], at_g(to)).start()
+
+    def hand_over(k):
+        block = wx.at[g_ahead[k], half]
+        push(block, block, hs, hr.at[k], at_g(g_ahead[k])).wait_recv()
+        push(block, block, ks, kr.at[k], {"dp_1": 1 - c}).start()
+
+    for k in EARLY:
+        fetch(k)
+
     own_rows = rows(d)
     pieces = [along(hop, 4, pair) for hop in HOPS]
     for j, i in enumerate(pieces):
@@ -256,6 +279,8 @@
         for which in range(2):
             pp[i, g, which, own_rows, :] = out[i, me, which]
     pre(18, 14)
+    for k in EARLY:
+        hand_over(k)
 
     def head(i, g_here):
         h = g_here * 4 + i
@@ -318,6 +343,8 @@
 
         lax.fori_loop(0, count // POST_HEADS, step, 0)
 
+    for k in LATE:
+        fetch(k)
     post(0, 8)
 
     for j in MID:
@@ -330,81 +357,35 @@
             gz[2 * i + 1, part, :] = summed[COLS:]
         for to in (mate,) if HOPS[j] == 0 else (2 * i, 2 * i + 1):
             push(gz.at[to], rz.at[along(to - z, 8, 0)], bs, br, at_z(to)).start()
+    for k in LATE:
+        hand_over(k)
     post(8, 8)
     grad = gz[z].astype(F32)
     drain(rz.at[pl.ds(1, 7)], br)
     for o in range(1, 8):
         grad += rz[o].astype(F32)
-    grad_high = grad.astype(BF16)
-    grad_low = (grad - grad_high.astype(F32)).astype(BF16)
-    grad_both = jnp.concatenate([grad_high, grad_low], axis=1)
-
-    def row_terms(half, at):
-        columns = pl.ds(pl.multiple_of(half * 2048 + at * 512, 512), 512)
-        terms = dot(w[:, columns], grad_both, TN)
-        terms = (terms[:, :128] + terms[:, 128:]).astype(BF16).reshape(8, 2, COLS // 2, 128)
-        for part in range(2):
-            rt[half, part, at] = terms[:, part]
-
-    def y_send(src, dst, landed, to):
-        push(src, dst, cs, landed, at_y(to)).start()
-
-    first, last = pl.ds(0, 4), pl.ds(4, 4)
-    chunks = [(n, half, part) for n, half in enumerate((other, x)) for part in range(2)]
-    for n, half in enumerate((other, x)):
-        row_terms(half, across)
-        for part in range(2):
-            y_send(rt.at[half, part, across, first], rl.at[n, part, 0], lr.at[n, part, 0], up)
-            y_send(rt.at[half, part, across, last], rl.at[n, part, 1], lr.at[n, part, 1], down)
-        row_terms(half, up)
-        for part in range(2):
-            y_send(rt.at[half, part, up, last], ry.at[n, part, 0, last], cr.at[n, part, 0], up)
-        row_terms(half, down)
-        for part in range(2):
-            y_send(rt.at[half, part, down, first], ry.at[n, part, 1, first], cr.at[n, part, 1], down)
-    for half in (other, x):
-        row_terms(half, y)
-
-    def y_add(n, half, part):
-        for way, to, piece in ((0, up, slice(0, 4)), (1, down, slice(4, 8))):
-            drain(rl.at[n, part, way], lr.at[n, part, way])
-            joined = rt[half, part, to, piece].astype(F32) + rl[n, part, way].astype(F32)
-            rt[half, part, to, piece] = joined.astype(BF16)
-            section = first if way == 0 else last
-            y_send(rt.at[half, part, to, section], ry.at[n, part, way, section], cr.at[n, part, way], to)
-
-    def y_sum(n, half, part):
-        three = rt[half, part, y].astype(F32)
-        for way in range(2):
-            drain(ry.at[n, part, way], cr.at[n, part, way])
-            three += ry[n, part, way].astype(F32)
-        t2[n, part] = three.astype(BF16)
-        for o in reversed(RING):
-            to = along(o, 8, z)
-            push(t2.at[n, part, to], rz2.at[n, part, o], es, er.at[n, part], at_z(to)).start()
-
-    def z_sum(n, part):
-        eight = t2[n, part, z].astype(F32)
-        drain(rz2.at[n, part, pl.ds(1, 7)], er.at[n, part])
-        for o in range(1, 8):
-            eight += rz2[n, part, o].astype(F32)
-        return eight
-
-    y_add(*chunks[0])
-    y_add(*chunks[1])
-    post(16, 6)
-    y_add(*chunks[2])
-    y_add(*chunks[3])
-    post(22, 10)
-    for chunk in chunks:
-        y_sum(*chunk)
+    gt[g] = grad.astype(BF16)
+
+    for k in range(1, 8):
+        push(gt.at[g], gt.at[g], cs, cr.at[k], at_g(g_behind[k])).start()
+    post(16, 10)
+    terms = dot(w[:, features(g)], gt[g], TN)
+    for k in range(1, 8):
+        source = g_ahead[k]
+        block = wx.at[source, missing]
+        push(block, block, ks, kr.at[k], {"dp_1": 1 - c}).wait_recv()
+        push(gt.at[source], gt.at[source], cs, cr.at[k], at_g(source)).wait_recv()
+        terms += dot(wx[source], gt[source], TN)
+    t2[...] = terms.astype(BF16).reshape(8, COLS, 128)
+    for o in reversed(RING):
+        to = along(o, 8, z)
+        push(t2.at[to], rz2.at[o], es, er, at_z(to)).start()
+    post(26, 6)
     mix = soft(logits[...])
-    for part in range(2):
-        sx[part * 32 : (part + 1) * 32] = z_sum(0, part)
-    push(sx, rx, fs, fr, x_peer).start()
-    mine = jnp.concatenate([z_sum(1, 0), z_sum(1, 1)], axis=0)
-    drain(rx, fr)
-    mixture_grad = mine + rx[...]
+    mixture_grad = t2[z].astype(F32)
+    drain(rz2.at[pl.ds(1, 7)], er)
+    for o in range(1, 8):
+        mixture_grad += rz2[o].astype(F32)
 
     flipped = mixture_grad.T
     part = jnp.zeros((NTASK, NSRC), F32)
@@ -434,9 +415,10 @@
     drain(out.at[:, pl.ds(0, PLANE - 1)], ps)
     drain(rg.at[:, pl.ds(0, PLANE - 1)], gs)
     drain(gz.at[pl.ds(0, 7)], bs)
-    drain(rt.at[:, :, pl.ds(0, 3)], cs)
-    drain(t2.at[:, :, pl.ds(0, 7)], es)
-    drain(sx, fs)
+    drain(wx.at[pl.ds(0, 7), half], hs)
+    drain(wx.at[pl.ds(0, 7), half], ks)
+    drain(gt.at[pl.ds(0, 7)], cs)
+    drain(t2.at[pl.ds(0, 7)], es)
     drain(wslot.at[pl.ds(0, PLANE - 1)], ws)
     drain(wz.at[pl.ds(0, 7)], vr)
     weight_grad = jnp.sum(wz[...], axis=0)
@@ -448,7 +430,6 @@
     any_space = pl.BlockSpec(memory_space=pl.ANY)
     vmem = pl.BlockSpec(memory_space=pltpu.VMEM)
     dma = pltpu.SemaphoreType.DMA
-    block = (8, COLS // 2, 128)
     attended, source_grad, logits_grad = pl.pallas_call(
         kernel,
         out_shape=(
@@ -461,6 +442,7 @@
         scratch_shapes=[
             pltpu.VMEM((ROWS, COLS, NSRC), BF16),
             pltpu.VMEM((2 * COLS, D), BF16),
+            pltpu.VMEM((8, 2 * COLS, 512), BF16),
             *[pltpu.VMEM((SEQ, D), BF16)] * 4,
             pltpu.VMEM((2, 4, 8, COLS, 128), BF16),
             pltpu.VMEM((8, 128, 128), BF16),
@@ -475,17 +457,14 @@
             pltpu.VMEM((4, PLANE, 2, ROWS, DH), BF16),
             pltpu.VMEM((8, 128, 128), BF16),
             pltpu.VMEM((8, 128, 128), BF16),
-            pltpu.VMEM((2, 2, 4, *block), BF16),
-            pltpu.VMEM((2, 2, 2, 4, COLS // 2, 128), BF16),
-            pltpu.VMEM((2, 2, 2, *block), BF16),
-            pltpu.VMEM((2, 2, *block), BF16),
-            pltpu.VMEM((2, 2, *block), BF16),
-            pltpu.VMEM((COLS, 128), F32),
-            pltpu.VMEM((COLS, 128), F32),
+            pltpu.VMEM((8, 128, 128), BF16),
+            pltpu.VMEM((8, COLS, 128), BF16),
+            pltpu.VMEM((8, COLS, 128), BF16),
             pltpu.VMEM((PLANE, NTASK, NSRC), F32),
             pltpu.VMEM((8, NTASK, NSRC), F32),
             dma((7,)), dma, dma((2, 8)), dma, dma, dma, dma((2, 2, 8)), dma, dma((2,)), dma, dma((8,)),
-            dma, dma, dma, dma((4, 8)), dma, dma((4,)), dma, dma, dma, dma((2, 2, 2)), dma((2, 2, 2)), dma, dma((2, 2)), dma, dma,
+            dma, dma, dma, dma((4, 8)), dma, dma((4,)), dma, dma((8,)), dma, dma((8,)),
+            dma, dma, dma, dma((8,)), dma, dma,
             dma, dma, dma, dma,
         ],
         compiler_params=pltpu.CompilerParams(collective_id=0, has_side_effects=True),

time: 94.4 us -> 86.8 us (0.919)
  Pallas kernels: 90.2 us -> 82.8 us
    pallas_call x1, Pallas kernels: 90.2 us -> 82.8 us  [on_device(): pl.pallas_call(kernel, out_shape=(pltpu.VMEM((SEQ, D), BF16), pltpu.VMEM(...]
where the time goes in v5:
time: 86.8 us; the launch traced here: 85.8 us
  Pallas kernels  82.8 us (95%)
  local copies, waits for them, and re-layouts  2.36 us (3%)
    pallas_call x1, Pallas kernels, on_device(): pl.pallas_call(kernel, out_shape=(pltpu.VMEM((SEQ, D), BF16), pltpu.VMEM(...  82.8 us
    unnamed x3, local copies, waits for them, and re-layouts  2.36 us

profile of v5, /device:TPU:8, one launch (start us, length us, event | category | flops | bytes accessed | tf_op | source)
XLA Modules:
  0.0 85.8 jit_solution(18378076514260784334)
XLA Ops:
  0.6 82.8 %prompt_step.1 = (bf16[128,4096]{1,0:T(8,128)(2,1)S(1)}, f32[16,64,128]{2,1,0:T(8,128)S(1)}, f32[8,128]{1,0:T(8,128)S(1)}) custom-call(s32[64]{0:T(128)} %tids.1, f32[8,128]{1,0:T(8,128)} %logits.1, bf16[64,64,128]{2,1,0:T(8,128)(2,1)} %bitcast.11, bf16[64,4096]{1,0:T(8,128)(2,1)} %bitcast.16, bf16[64,4096]{1,0:T(8,128)(2,1)} %bitcast.17, ...), custom_call_target="tpu_custom_call" | custom-call | tf_op jit(solution)/shard_map/prompt_step/pallas_call | solution.py:433
  83.5 1.0 %copy.15 = bf16[1,128,4096]{2,1,0:T(8,128)(2,1)} copy(bf16[1,128,4096]{2,1,0:T(8,128)(2,1)S(1)} %bitcast.9) | data formatting | bytes 2097152
  84.4 0.8 copy.16
  85.2 0.6 copy.17

commit v6 on v5

--- a/solution.py
+++ b/solution.py
@@ -56,6 +56,7 @@
 HOPS = (0, 1, 3, 2)
 MID = (1, 2, 3, 0)
 RING = (1, 7, 2, 6, 3, 5, 4)
+NEAR = (4, 1, 7, 3, 5, 2, 6)
 EARLY, LATE = (1, 7, 4, 3), (2, 6, 5)
 PRE_HEADS = 2
 MID_HEADS = 2
@@ -242,7 +243,7 @@
         for one in (mate,) if hop == 0 else (2 * to, 2 * to + 1):
             u_send(one)
 
-    half = pl.ds(pl.multiple_of(c * COLS, COLS), COLS)
+    mine = pl.ds(pl.multiple_of(c * COLS, COLS), COLS)
     missing = pl.ds(pl.multiple_of((1 - c) * COLS, COLS), COLS)
 
     def features(at):
@@ -250,10 +251,10 @@
 
     def fetch(k):
         to = g_behind[k]
-        push(w.at[half, features(to)], wx.at[g, half], hs, hr.at[k], at_g(to)).start()
+        push(w.at[mine, features(to)], wx.at[g, mine], hs, hr.at[k], at_g(to)).start()
 
     def hand_over(k):
-        block = wx.at[g_ahead[k], half]
+        block = wx.at[g_ahead[k], mine]
         push(block, block, hs, hr.at[k], at_g(g_ahead[k])).wait_recv()
         push(block, block, ks, kr.at[k], {"dp_1": 1 - c}).start()
 
@@ -366,11 +367,11 @@
         grad += rz[o].astype(F32)
     gt[g] = grad.astype(BF16)
 
-    for k in range(1, 8):
+    for k in reversed(NEAR):
         push(gt.at[g], gt.at[g], cs, cr.at[k], at_g(g_behind[k])).start()
     post(16, 10)
     terms = dot(w[:, features(g)], gt[g], TN)
-    for k in range(1, 8):
+    for k in NEAR:
         source = g_ahead[k]
         block = wx.at[source, missing]
         push(block, block, ks, kr.at[k], {"dp_1": 1 - c}).wait_recv()
@@ -388,11 +389,15 @@
         mixture_grad += rz2[o].astype(F32)
 
     flipped = mixture_grad.T
-    part = jnp.zeros((NTASK, NSRC), F32)
+    high = flipped.astype(BF16).astype(F32)
+    middle = (flipped - high).astype(BF16).astype(F32)
+    low = flipped - high - middle
+    part = jnp.zeros((4 * NTASK, NSRC), F32)
     for r in range(ROWS):
-        part += jnp.dot(
-            flipped[r * NTASK : (r + 1) * NTASK], spv[r].astype(F32), precision=HIGH, preferred_element_type=F32
-        )
+        these = slice(r * NTASK, (r + 1) * NTASK)
+        terms = jnp.concatenate([high[these], middle[these], low[these], jnp.zeros_like(low[these])], axis=0)
+        part += dot(terms.astype(BF16), spv[r])
+    part = part[:NTASK] + part[NTASK : 2 * NTASK] + part[2 * NTASK : 3 * NTASK]
     wslot[me] = part
 
     for k, dd in partners:
@@ -415,8 +420,8 @@
     drain(out.at[:, pl.ds(0, PLANE - 1)], ps)
     drain(rg.at[:, pl.ds(0, PLANE - 1)], gs)
     drain(gz.at[pl.ds(0, 7)], bs)
-    drain(wx.at[pl.ds(0, 7), half], hs)
-    drain(wx.at[pl.ds(0, 7), half], ks)
+    drain(wx.at[pl.ds(0, 7), mine], hs)
+    drain(wx.at[pl.ds(0, 7), mine], ks)
     drain(gt.at[pl.ds(0, 7)], cs)
     drain(t2.at[pl.ds(0, 7)], es)
     drain(wslot.at[pl.ds(0, PLANE - 1)], ws)

time: 86.8 us -> 86.5 us (level)
  no operation moved by 1% of the time
where the time goes in v6:
time: 86.5 us; the launch traced here: 85.2 us
  Pallas kernels  82.2 us (95%)
  local copies, waits for them, and re-layouts  2.36 us (3%)
    pallas_call x1, Pallas kernels, on_device(): pl.pallas_call(kernel, out_shape=(pltpu.VMEM((SEQ, D), BF16), pltpu.VMEM(...  82.2 us
    unnamed x3, local copies, waits for them, and re-layouts  2.36 us

profile of v6, /device:TPU:8, one launch (start us, length us, event | category | flops | bytes accessed | tf_op | source)
XLA Modules:
  0.0 85.2 jit_solution(3172143801091936810)
XLA Ops:
  0.6 82.2 %prompt_step.1 = (bf16[128,4096]{1,0:T(8,128)(2,1)S(1)}, f32[16,64,128]{2,1,0:T(8,128)S(1)}, f32[8,128]{1,0:T(8,128)S(1)}) custom-call(s32[64]{0:T(128)} %tids.1, f32[8,128]{1,0:T(8,128)} %logits.1, bf16[64,64,128]{2,1,0:T(8,128)(2,1)} %bitcast.11, bf16[64,4096]{1,0:T(8,128)(2,1)} %bitcast.16, bf16[64,4096]{1,0:T(8,128)(2,1)} %bitcast.17, ...), custom_call_target="tpu_custom_call" | custom-call | tf_op jit(solution)/shard_map/prompt_step/pallas_call | solution.py:438
  82.8 1.0 %copy.15 = bf16[1,128,4096]{2,1,0:T(8,128)(2,1)} copy(bf16[1,128,4096]{2,1,0:T(8,128)(2,1)S(1)} %bitcast.9) | data formatting | bytes 2097152
  83.8 0.8 copy.16
  84.6 0.6 copy.17

commit v7 on v6

--- a/solution.py
+++ b/solution.py
@@ -429,6 +429,28 @@
     weight_grad = jnp.sum(wz[...], axis=0)
     logits_grad[...] = mix * (weight_grad - jnp.sum(mix * weight_grad, axis=1, keepdims=True))
     drain(wz.at[pl.ds(0, 7)], vs)
+
+
+def finish_kernel(attended, source_grad, logits_grad, attended_out, source_out, logits_out, sems):
+    given = ((attended, attended_out), (source_grad, source_out), (logits_grad, logits_out))
+    copies = [pltpu.make_async_copy(one, to, sems.at[n]) for n, (one, to) in enumerate(given)]
+    for one in copies:
+        one.start()
+    for one in copies:
+        one.wait()
+
+
+def finish(*given):
+    vmem = pl.BlockSpec(memory_space=pltpu.VMEM)
+    any_space = pl.BlockSpec(memory_space=pl.ANY)
+    return pl.pallas_call(
+        finish_kernel,
+        out_shape=tuple(jax.ShapeDtypeStruct(one.shape, one.dtype) for one in given),
+        in_specs=[vmem] * 3,
+        out_specs=(any_space,) * 3,
+        scratch_shapes=[pltpu.SemaphoreType.DMA((3,))],
+        name="prompt_finish",
+    )(*(pltpu.with_memory_space_constraint(one, pltpu.VMEM) for one in given))
 
 
 def on_device(source_prompts, task_logits, task_ids, key_weight, value_weight, queries, keys, values, cotangent):
@@ -478,6 +500,7 @@
         task_ids, task_logits, source_prompts.transpose(1, 2, 0), key_weight.T, value_weight.T,
         queries[0], keys[0], values[0], cotangent[0],
     )
+    attended, source_grad, logits_grad = finish(attended, source_grad, logits_grad)
     return attended[None], source_grad.transpose(2, 0, 1), logits_grad
 
 

time: 86.5 us -> 85.3 us (0.986)
  local copies, waits for them, and re-layouts: 2.36 us -> 0 us
  Pallas kernels: 82.2 us -> 83.4 us
    unnamed x3 -> x0, local copies, waits for them, and re-layouts: 2.36 us -> none
    pallas_call x0 -> x1, Pallas kernels: none -> 1.17 us  [finish(): pl.pallas_call(finish_kernel, out_shape=tuple((jax.ShapeDtypeStruct(one.s...]
where the time goes in v7:
time: 85.3 us; the launch traced here: 84 us
  Pallas kernels  83.4 us (98%)
    pallas_call x1, Pallas kernels, on_device(): pl.pallas_call(kernel, out_shape=(pltpu.VMEM((SEQ, D), BF16), pltpu.VMEM(...  82.2 us

profile of v7, /device:TPU:8, one launch (start us, length us, event | category | flops | bytes accessed | tf_op | source)
XLA Modules:
  0.0 84.0 jit_solution(12523727607491018002)
XLA Ops:
  0.6 82.2 %prompt_step.1 = (bf16[128,4096]{1,0:T(8,128)(2,1)S(1)}, f32[16,64,128]{2,1,0:T(8,128)S(1)}, f32[8,128]{1,0:T(8,128)S(1)}) custom-call(s32[64]{0:T(128)} %tids.1, f32[8,128]{1,0:T(8,128)} %logits.1, bf16[64,64,128]{2,1,0:T(8,128)(2,1)} %bitcast.9, bf16[64,4096]{1,0:T(8,128)(2,1)} %bitcast.14, bf16[64,4096]{1,0:T(8,128)(2,1)} %bitcast.15, ...), custom_call_target="tpu_custom_call" | custom-call | tf_op jit(solution)/shard_map/prompt_step/pallas_call | solution.py:460
  82.8 1.2 %prompt_finish.1 = (bf16[128,4096]{1,0:T(8,128)(2,1)}, f32[16,64,128]{2,1,0:T(8,128)}, f32[8,128]{1,0:T(8,128)}) custom-call(bf16[128,4096]{1,0:T(8,128)(2,1)S(1)} %get-tuple-element.9.attended, f32[16,64,128]{2,1,0:T(8,128)S(1)} %get-tuple-element.10.source_grad, f32[8,128]{1,0:T(8,128)S(1)} %get-tuple-element.11.logits_grad), custom_call_target="tpu_custom_call" | custom-call | tf_op jit(solution)/shard_map/prompt_finish/pallas_call | solution.py:446

commit v8 on v7

--- a/solution.py
+++ b/solution.py
@@ -59,7 +59,7 @@
 NEAR = (4, 1, 7, 3, 5, 2, 6)
 EARLY, LATE = (1, 7, 4, 3), (2, 6, 5)
 PRE_HEADS = 2
-MID_HEADS = 2
+MID_HEADS = 4
 POST_HEADS = 2
 
 

time: 85.3 us -> 86.2 us (1.011)
  Pallas kernels: 83.4 us -> 84.4 us
    pallas_call x1, Pallas kernels: 82.2 us -> 83.3 us  [on_device(): pl.pallas_call(kernel, out_shape=(pltpu.VMEM((SEQ, D), BF16), pltpu.VMEM(...]
where the time goes in v8:
time: 86.2 us; the launch traced here: 85.1 us
  Pallas kernels  84.4 us (98%)
    pallas_call x1, Pallas kernels, on_device(): pl.pallas_call(kernel, out_shape=(pltpu.VMEM((SEQ, D), BF16), pltpu.VMEM(...  83.3 us

profile of v8, /device:TPU:8, one launch (start us, length us, event | category | flops | bytes accessed | tf_op | source)
XLA Modules:
  0.0 85.1 jit_solution(7594586039396017144)
XLA Ops:
  0.6 83.3 %prompt_step.1 = (bf16[128,4096]{1,0:T(8,128)(2,1)S(1)}, f32[16,64,128]{2,1,0:T(8,128)S(1)}, f32[8,128]{1,0:T(8,128)S(1)}) custom-call(s32[64]{0:T(128)} %tids.1, f32[8,128]{1,0:T(8,128)} %logits.1, bf16[64,64,128]{2,1,0:T(8,128)(2,1)} %bitcast.9, bf16[64,4096]{1,0:T(8,128)(2,1)} %bitcast.14, bf16[64,4096]{1,0:T(8,128)(2,1)} %bitcast.15, ...), custom_call_target="tpu_custom_call" | custom-call | tf_op jit(solution)/shard_map/prompt_step/pallas_call | solution.py:460
  83.9 1.2 %prompt_finish.1 = (bf16[128,4096]{1,0:T(8,128)(2,1)}, f32[16,64,128]{2,1,0:T(8,128)}, f32[8,128]{1,0:T(8,128)}) custom-call(bf16[128,4096]{1,0:T(8,128)(2,1)S(1)} %get-tuple-element.9.attended, f32[16,64,128]{2,1,0:T(8,128)S(1)} %get-tuple-element.10.source_grad, f32[8,128]{1,0:T(8,128)S(1)} %get-tuple-element.11.logits_grad), custom_call_target="tpu_custom_call" | custom-call | tf_op jit(solution)/shard_map/prompt_finish/pallas_call | solution.py:446
